TPU v7x, 256 devices: a whole 4x4x8 slice. The times are simulated.
256 devices in a mesh: dp: 32 (over z_lo, x, y), tensor: 8 (over z_hi, core).
Axes of the slice: x: 4, y: 4, z: 8 (z_hi: 4, z_lo: 2; z = z_hi * 2 + z_lo), core: 2. Of those that a mesh axis runs over, the one named last changes fastest.
Arguments:
- hidden: bfloat16 [4096, 8192], P('dp')
- q_weight: float32 [8192, 4096], P(('dp', 'tensor')), may hold values from -0.0625 to 0.0625
- k_weight: float32 [8192, 1024], P(('dp', 'tensor')), may hold values from -0.0625 to 0.0625
- v_weight: float32 [8192, 1024], P(('dp', 'tensor')), may hold values from -0.0625 to 0.0625
- o_weight: float32 [8192, 4096], P(('dp', 'tensor')), may hold values from -0.09375 to 0.09375
- input_gain: float32 [8192], replicated, may hold values from 0.25 to 1.75
- post_gain: float32 [8192], replicated, may hold values from 0.25 to 1.75
- key_cache: bfloat16 [4096, 64, 8, 128], P('dp', None, 'tensor'), may hold values from -1000 to 1000
- value_cache: bfloat16 [4096, 64, 8, 128], P('dp', None, 'tensor'), may hold values from -6 to 6
- lengths: int32 [4096], P('dp'), may hold values from 1 to 64
Outputs:
- new_hidden: bfloat16 [4096, 8192], P('dp')
- normed: bfloat16 [4096, 8192], P('dp')
- fresh_token_keys: bfloat16 [4096, 8, 128], P('dp', 'tensor')
- new_values: bfloat16 [4096, 8, 128], P('dp', 'tensor')
All inputs are finite; a program needn't handle non-finite values.
Results may differ from a plain program's by a relative error of at most 0.012.
The roundings to bfloat16 on the way count: a program that leaves them out, or rounds other values in their place, can miss the bound.
Values may be sent and summed in bfloat16 or wider, within the bound.
No kernel may reach another device: no remote copies, remote signals or barrier semaphores. Data moves between devices by JAX's collectives and lax.ppermute only.
A program may use at most 128 MiB of HBM per device.

v0:
```python
import math

import jax
import jax.numpy as jnp
from jax import lax
from jax.sharding import PartitionSpec as P

HEADS = 32
KV_HEADS = 8
HEAD_DIM = 128


epsilon = 1e-05
rope_base = 500000.0


def side_by_side(arrays, axis, dim, along):
    ends, at = ([], 0)
    for a in arrays[:-1]:
        at += a.shape[along]
        ends.append(at)
    both = jnp.concatenate(arrays, axis=along)
    return tuple(jnp.split(lax.all_gather(both, axis, axis=dim, tiled=True), ends, axis=along))


def rms_gain(values, gain_vector):
    mean_square = jnp.mean(values * values, axis=-1, keepdims=True)
    return values * lax.rsqrt(mean_square + epsilon) * gain_vector


def rotate(values, positions):
    half_dim = values.shape[-1] // 2
    index_row = jnp.arange(half_dim, dtype=jnp.float32)
    frequency = jnp.exp(-math.log(rope_base) * index_row / half_dim)
    angle = positions.astype(jnp.float32)[:, None, None] * frequency[None, None, :]
    first_half = values[..., :half_dim]
    second_half = values[..., half_dim:]
    return jnp.concatenate(
        [
            first_half * jnp.cos(angle) - second_half * jnp.sin(angle),
            second_half * jnp.cos(angle) + first_half * jnp.sin(angle),
        ],
        axis=-1,
    )


def attend(query_b, fresh_token_keys, new_values, key_cache, value_cache, lengths):
    row_count, kv_count = (fresh_token_keys.shape[0], fresh_token_keys.shape[1])
    grouped_heads = query_b.reshape(row_count, kv_count, -1, HEAD_DIM)
    reciprocal_root = 1.0 / math.sqrt(HEAD_DIM)
    scores = (
        jnp.einsum("bkgd,blkd->bkgl", grouped_heads, key_cache, preferred_element_type=jnp.float32)
        * reciprocal_root
    )
    self_token_score = (
        jnp.einsum(
            "lfxa,lfa->lfx", grouped_heads, fresh_token_keys, preferred_element_type=jnp.float32
        )
        * reciprocal_root
    )
    visible = jnp.arange(key_cache.shape[1], dtype=jnp.int32)[None, :] < lengths[:, None]
    scores = jnp.where(visible[:, None, None, :], scores, -jnp.inf)
    largest = jnp.maximum(jnp.max(scores, axis=-1), self_token_score)
    kept_exp = jnp.exp(scores - largest[..., None])
    own_exp = jnp.exp(self_token_score - largest)
    softmax_divisor = jnp.sum(kept_exp, axis=-1) + own_exp
    weights_kept = (kept_exp / softmax_divisor[..., None]).astype(jnp.bfloat16)
    own_weight = (own_exp / softmax_divisor).astype(jnp.bfloat16)
    attended = jnp.einsum(
        "bkgl,blkd->bkgd", weights_kept, value_cache, preferred_element_type=jnp.float32
    )
    attended = (
        attended
        + own_weight.astype(jnp.float32)[..., None] * new_values.astype(jnp.float32)[:, :, None, :]
    )
    return attended.reshape(row_count, -1).astype(jnp.bfloat16)


def shards(
    hidden,
    q_weight,
    k_weight,
    v_weight,
    o_weight,
    input_gain,
    post_gain,
    key_cache,
    value_cache,
    lengths,
):
    tensor_size = lax.axis_size("tensor")
    row_count = hidden.shape[0]
    heads_here = HEADS // tensor_size
    kv_here = KV_HEADS // tensor_size
    w_query, w_key, value_matrix, w_out = (
        lax.all_to_all(
            q_weight.astype(jnp.bfloat16), "tensor", split_axis=1, concat_axis=0, tiled=True
        ),
        lax.all_to_all(
            k_weight.astype(jnp.bfloat16), "tensor", split_axis=1, concat_axis=0, tiled=True
        ),
        lax.all_to_all(
            v_weight.astype(jnp.bfloat16), "tensor", split_axis=1, concat_axis=0, tiled=True
        ),
        lax.all_to_all(
            o_weight.astype(jnp.bfloat16), "tensor", split_axis=1, concat_axis=0, tiled=True
        ),
    )
    normal_in = rms_gain(hidden.astype(jnp.float32), input_gain).astype(jnp.bfloat16)
    portions = side_by_side((w_query, w_key, value_matrix), "dp", 0, 1)
    query, key_part, value_part = tuple(
        (jnp.dot(normal_in, portion, preferred_element_type=jnp.float32) for portion in portions)
    )
    query_b = rotate(query.reshape(row_count, heads_here, HEAD_DIM), lengths).astype(jnp.bfloat16)
    fresh_token_keys = rotate(key_part.reshape(row_count, kv_here, HEAD_DIM), lengths).astype(
        jnp.bfloat16
    )
    new_values = value_part.reshape(row_count, kv_here, HEAD_DIM).astype(jnp.bfloat16)
    attended = attend(query_b, fresh_token_keys, new_values, key_cache, value_cache, lengths)
    partial_value = lax.dot_general(
        attended,
        lax.all_gather(w_out, "dp", axis=0, tiled=True),
        (((1,), (1,)), ((), ())),
        preferred_element_type=jnp.float32,
    )
    mixed = lax.psum(partial_value.astype(jnp.bfloat16), "tensor").astype(jnp.float32)
    residual = hidden.astype(jnp.float32) + mixed
    new_hidden = residual.astype(jnp.bfloat16)
    normed = rms_gain(residual, post_gain).astype(jnp.bfloat16)
    return (new_hidden, normed, fresh_token_keys, new_values)


def solution(mesh):
    in_specs = (
        P("dp", None),
        P(("dp", "tensor"), None),
        P(("dp", "tensor"), None),
        P(("dp", "tensor"), None),
        P(("dp", "tensor"), None),
        P(),
        P(),
        P("dp", None, "tensor", None),
        P("dp", None, "tensor", None),
        P("dp"),
    )
    out_specs = (P("dp", None), P("dp", None), P("dp", "tensor", None), P("dp", "tensor", None))
    return jax.shard_map(shards, mesh=mesh, in_specs=in_specs, out_specs=out_specs, check_vma=False)
```

profile of v0, /device:TPU:2, one launch (start us, length us, event | category | flops | bytes accessed | tf_op | source)
XLA Modules:
  0.0 504.1 jit_solution(8640591926322045796)
XLA Ops:
  7.2 1.7 copy_bitcast_fusion.3
  8.9 8.5 %all-to-all-start.1 = ((bf16[32,8,128]{2,0,1:T(8,128)(2,1)}), bf16[32,8,128]{2,0,1:T(8,128)(2,1)S(1)}, u32[]{:S(2)}, u32[]{:S(2)}) async-start(bf16[32,8,128]{2,0,1:T(8,128)(2,1)} %copy_bitcast_fusion.3), calls=%async_computation.1 | async-start | bytes 131072 | tf_op jit(solution)/shard_map/all_to_all | solution.py:99
  17.4 1.5 copy_bitcast_fusion.2
  18.9 6.8 %all-to-all-done.1 = bf16[32,8,128]{2,0,1:T(8,128)(2,1)S(1)} async-done(((bf16[32,8,128]{2,0,1:T(8,128)(2,1)}), bf16[32,8,128]{2,0,1:T(8,128)(2,1)S(1)}, u32[]{:S(2)}, u32[]{:S(2)}) %all-to-all-start.1) | async-done | bytes 65568 | tf_op jit(solution)/shard_map/all_to_all | solution.py:99
  25.7 3.4 all-to-all-start.2
  29.1 1.1 convert_element_type.79
  30.2 7.1 %all-to-all-done.2 = bf16[32,8,128]{2,0,1:T(8,128)(2,1)S(1)} async-done(((bf16[32,8,128]{2,0,1:T(8,128)(2,1)}), bf16[32,8,128]{2,0,1:T(8,128)(2,1)S(1)}, u32[]{:S(2)}, u32[]{:S(2)}) %all-to-all-start.2) | async-done | bytes 65568 | tf_op jit(solution)/shard_map/all_to_all | solution.py:102
  37.3 14.8 %all_to_all.76 = bf16[32,8,512]{2,0,1:T(8,128)(2,1)S(1)} all-to-all(bf16[32,8,512]{2,0,1:T(8,128)(2,1)S(1)} %bitcast.62), channel_id=1, replica_groups=mesh['dp'=32,'tensor'=8] {'tensor'}, dimensions={1} | all-to-all | bytes 524288 | tf_op jit(solution)/shard_map/all_to_all | solution.py:96
  52.1 0.8 pad_maximum_fusion
  53.0 1.1 convert_element_type.90
  54.1 14.4 %all_to_all.77 = bf16[32,8,512]{2,0,1:T(8,128)(2,1)} all-to-all(bf16[32,8,512]{2,0,1:T(8,128)(2,1)S(1)} %bitcast.63), channel_id=1, replica_groups=mesh['dp'=32,'tensor'=8] {'tensor'}, dimensions={1} | all-to-all | bytes 524288 | tf_op jit(solution)/shard_map/all_to_all | solution.py:105
  68.6 2.1 fusion.2
  71.1 152.6 %all-gather.3.cloned.1.call-done = bf16[8192,768]{1,0:T(8,128)(2,1)} async-done(((bf16[256,768]{1,0:T(8,128)(2,1)}), bf16[8192,768]{1,0:T(8,128)(2,1)}) %all-gather.3.cloned.1.call-update) | async-done | bytes 12582928 | tf_op jit(solution)/shard_map/all_gather | solution.py:23
  223.7 3.3 fusion.26
  227.3 5.3 %fusion = f32[128,512]{1,0:T(8,128)S(1)} fusion(bf16[8192,768]{1,0:T(8,128)(2,1)} %all-gather.3.cloned.1.call-done, bf16[128,8192]{1,0:T(8,128)(2,1)} %param.10, f32[8192]{0:T(1024)S(1)} %copy-done.5, f32[128]{0:T(128)S(1)} %add_rsqrt_fusion.1), kind=kOutput, calls=%fused_computation.1 | convolution fusion | flops 1077936128 | bytes 10781184 | tf_op jit(solution)/shard_map/dot_general | solution.py:112
  233.5 2.9 fusion.51
  237.3 3.7 fusion.50
  241.0 0.7 fusion.23
  241.7 150.4 %all-gather.5.cloned.1.call-done = bf16[8192,512]{1,0:T(8,128)(2,1)} async-done(((bf16[256,512]{1,0:T(8,128)(2,1)}), bf16[8192,512]{1,0:T(8,128)(2,1)}) %all-gather.5.cloned.1.call-update) | async-done | bytes 8388624 | tf_op jit(solution)/shard_map/all_gather | solution.py:122
  392.1 7.5 %convolution_convert_fusion = bf16[128,8192]{1,0:T(8,128)(2,1)} fusion(bf16[8192,512]{1,0:T(8,128)(2,1)} %all-gather.5.cloned.1.call-done, bf16[16,8,4,128]{3,2,1,0:T(4,128)(2,1)S(1)} %bitcast.68), kind=kOutput, calls=%fused_computation | convolution fusion | flops 1074790400 | bytes 10616832 | tf_op jit(solution)/shard_map/dot_general | solution.py:120
  399.7 0.7 copy.43
  400.4 90.4 %all-reduce.2.cloned.1.call-done = bf16[128,8192]{1,0:T(8,128)(2,1)} async-done(((bf16[128,8192]{1,0:T(8,128)(2,1)}), bf16[128,8192]{1,0:T(8,128)(2,1)}) %all-reduce.2.cloned.1.call-update) | async-done | bytes 2097168 | tf_op jit(solution)/shard_map/psum | solution.py:126
  490.8 3.1 multiply_reduce_fusion
  494.3 3.2 multiply_convert_fusion
  (42 shorter events, 2.9 us)
Async XLA Ops:
  7.2 233.8 %copy-start = (bf16[128,64,1,128]{3,1,2,0:T(8,128)(2,1)S(1)}, bf16[128,64,1,128]{3,1,2,0:T(8,128)(2,1)}, u32[]{:S(2)}) copy-start(bf16[128,64,1,128]{3,1,2,0:T(8,128)(2,1)} %param.18) | copy-start | bytes 6291460
  7.2 61.4 %copy-start.4 = (s32[128]{0:T(128)S(1)}, s32[128]{0:T(128)}, u32[]{:S(2)}) copy-start(s32[128]{0:T(128)} %param.19) | copy-start | bytes 1540
  7.2 216.5 %copy-start.5 = (f32[8192]{0:T(1024)S(1)}, f32[8192]{0:T(1024)}, u32[]{:S(2)}) copy-start(f32[8192]{0:T(1024)} %param.15) | copy-start | bytes 98308
  8.9 16.8 %all-to-all-start.1 = ((bf16[32,8,128]{2,0,1:T(8,128)(2,1)}), bf16[32,8,128]{2,0,1:T(8,128)(2,1)S(1)}, u32[]{:S(2)}, u32[]{:S(2)}) async-start(bf16[32,8,128]{2,0,1:T(8,128)(2,1)} %copy_bitcast_fusion.3), calls=%async_computation.1 | async-start | bytes 131072 | tf_op jit(solution)/shard_map/all_to_all | solution.py:99
  25.7 11.6 %all-to-all-start.2 = ((bf16[32,8,128]{2,0,1:T(8,128)(2,1)}), bf16[32,8,128]{2,0,1:T(8,128)(2,1)S(1)}, u32[]{:S(2)}, u32[]{:S(2)}) async-start(bf16[32,8,128]{2,0,1:T(8,128)(2,1)} %copy_bitcast_fusion.2), calls=%async_computation.2 | async-start | bytes 131072 | tf_op jit(solution)/shard_map/all_to_all | solution.py:102
  29.1 194.7 %all-gather.3.cloned.1.call-start = ((), (), s32[]{:S(2)}) async-start(), calls=%async_computation.4 | async-start | bytes 12976128 | tf_op jit(solution)/shard_map/all_gather | solution.py:23
  52.9 339.2 %all-gather.5.cloned.1.call-start = ((), (), s32[]{:S(2)}) async-start(), calls=%async_computation.5 | async-start | bytes 8650752 | tf_op jit(solution)/shard_map/all_gather | solution.py:122
  68.5 422.3 %all-reduce.2.cloned.1.call-start = ((), (), s32[]{:S(2)}) async-start(), calls=%async_computation.6 | async-start | bytes 4194304 | tf_op jit(solution)/shard_map/psum | solution.py:126
  399.6 94.3 %copy-start.3 = (f32[8192]{0:T(1024)S(1)}, f32[8192]{0:T(1024)}, u32[]{:S(2)}) copy-start(f32[8192]{0:T(1024)} %param.16) | copy-start | bytes 98308
  490.8 3.2 copy-start.1
  490.8 3.5 copy-start.2
Sparse Core Ops, SparseCore 0:
  53.0 170.6 all-gather.2
  225.5 166.5 all-gather.4
  399.8 90.9 all-reduce.1
where the time goes:
time: 505 us; the launch traced here: 504 us
  waiting for transfers between devices  407 us (81%)
  blocking collectives  29.2 us (6%)
  matrix products  23.5 us (5%)
  other arithmetic  16.3 us (3%)
  between operations  14 us (3%)
  starting transfers between devices  11.9 us (2%)
    all_gather x1, waiting for transfers between devices, side_by_side(): lax.all_gather(both, axis, axis=dim, tiled=True)  153 us
    all_gather x1, waiting for transfers between devices, shards(): lax.all_gather(w_out, 'dp', axis=0, tiled=True)  150 us
    psum x1, waiting for transfers between devices, shards(): lax.psum(partial_value.astype(jnp.bfloat16), 'tensor').astype(jnp.float32)  90.4 us
    all_to_all x1, blocking collectives, shards(): lax.all_to_all(q_weight.astype(jnp.bfloat16), 'tensor', split_axis=1, con...  14.8 us
    all_to_all x1, blocking collectives, shards(): lax.all_to_all(o_weight.astype(jnp.bfloat16), 'tensor', split_axis=1, con...  14.4 us
    dot_general x3, matrix products, shards(): jnp.dot(normal_in, portion, preferred_element_type=jnp.float32)  12.3 us
  transfers between devices with their start and end apart: 5, of which 5 were waited for; matrix products, arithmetic and copies ran while one was open for 5% of the time, Pallas kernels for 0%

commit v1 on v0

v1 whole, which is shorter than its diff:
```python
import math

import jax
import jax.numpy as jnp
from jax import lax
from jax.experimental import pallas as pl
from jax.experimental.pallas import tpu as pltpu
from jax.sharding import Mesh
from jax.sharding import PartitionSpec as P


HEAD_DIM = 128
ROWS = 128
D = 8192
CUT = 1024

epsilon = 1e-05
rope_base = 500000.0


bf16, f32 = jnp.bfloat16, jnp.float32
VM = pl.BlockSpec(memory_space=pltpu.VMEM)
SM = pl.BlockSpec(memory_space=pltpu.SMEM)


def shift(value, axis, size, step):
    return lax.ppermute(value, axis, [(i, (i + step) % size) for i in range(size)])


def cut_kernel(q, k, v, out):
    for t in range(8):
        out[t, :, 0:512] = q[:, t * 512 : t * 512 + 512].astype(bf16)
        out[t, :, 512:640] = k[:, t * 128 : t * 128 + 128].astype(bf16)
        out[t, :, 640:768] = v[:, t * 128 : t * 128 + 128].astype(bf16)


def norm_kernel(idx, hid, gain, own, send1, send2, send3, scale):
    zl, x, y, c = idx[0], idx[1], idx[2], idx[4]

    def add(j, total):
        part = hid[:, pl.ds(pl.multiple_of(j * 1024, 1024), 1024)].astype(f32)
        return total + jnp.sum(part * part, axis=-1, keepdims=True)

    total = lax.fori_loop(0, 8, add, jnp.zeros((ROWS, 1), f32))
    scale[...] = jnp.broadcast_to(lax.rsqrt(total / D + epsilon), (ROWS, 128))

    def step(j, carry):
        zs, xs = j // 4, j % 4
        there = ((zl ^ zs) * 4 + (x + 4 - xs) % 4) * 4
        to = pl.ds(pl.multiple_of(j * 256, 256), 256)
        for ys, out in ((1, send1), (2, send2), (3, send3), (0, own)):
            cols = pl.ds(pl.multiple_of((there + (y + ys) % 4) * 256, 256), 256)
            g = gain[:, cols]
            for cr in range(1 if ys else 2):
                rows = pl.ds(pl.multiple_of((c ^ cr) * 64, 64), 64)
                value = hid[rows, cols].astype(f32) * scale[rows, 0:1] * g
                if ys:
                    out[:, to] = value.astype(bf16)
                else:
                    out[cr, :, to] = value.astype(bf16)
        return carry

    lax.fori_loop(0, 8, step, 0)


def left_rows(h0, hown, hpart, ks):
    rows = [h0[0, :, ks], h0[1, :, ks]]
    for s in range(3):
        rows += [hown[s][:, ks], hpart[s, :, ks]]
    return jnp.concatenate(rows, axis=0)


def first_kernel(h0, ha, hb, hc, hpart, w0, w1, w3, v0, acc):
    def step(n, carry):
        cols = pl.ds(pl.multiple_of(n * 256, 256), 256)
        part = jnp.zeros((512, 256), f32)
        for k, w in ((0, w0), (1, w1), (3, w3), (4, v0)):
            lhs = left_rows(h0, (ha, hb, hc), hpart, slice(k * 256, k * 256 + 256))
            part = part + jnp.dot(lhs, w[:, cols], preferred_element_type=f32)
        acc[:, cols] = part
        return carry

    lax.fori_loop(0, 3, step, 0)


def second_kernel(h0, ha, hb, hc, hpart, v1, v3, wa, wb, va, vb, acc, p0, p1, p2, p3):
    def step(n, carry):
        cols = pl.ds(pl.multiple_of(n * 256, 256), 256)
        part = acc[:, cols]
        for k, w in ((5, (v1,)), (7, (v3,)), (2, (wa, wb)), (6, (va, vb))):
            lhs = left_rows(h0, (ha, hb, hc), hpart, slice(k * 256, k * 256 + 256))
            rhs = jnp.concatenate([r[:, cols] for r in w], axis=0)
            part = part + jnp.dot(lhs, rhs, preferred_element_type=f32)
        for s, p in enumerate((p0, p1, p2, p3)):
            p[:, cols] = part[s * 128 : (s + 1) * 128].astype(p.dtype)
        return carry

    lax.fori_loop(0, 3, step, 0)


def attend_kernel(idx, p0, r1, r2, r3, cos, sin, lengths, keys, vals, att, fresh, newv, qkv, qs, fs, vs, sc, out):
    c = idx[4]
    total = p0[...] + r1[...].astype(f32) + r2[...].astype(f32) + r3[...].astype(f32)
    qkv[pl.ds(pl.multiple_of(c * 64, 64), 64)] = total[:64]
    qkv[pl.ds(pl.multiple_of(64 - c * 64, 64), 64)] = total[64:]

    def turn(v):
        return (v * cos[...] + pltpu.roll(v, 64, 1) * sin[...]).astype(bf16)

    fk = turn(qkv[:, 512:640])
    nv = qkv[:, 640:768].astype(bf16)
    fresh[...] = fk
    newv[...] = nv
    fs[...] = fk.astype(f32).reshape(16, 8, 128)
    vs[...] = nv.astype(f32).reshape(16, 8, 128)
    for h in range(4):
        qs[:, h] = turn(qkv[:, h * 128 : h * 128 + 128]).astype(f32).reshape(16, 8, 128)
    root = 1.0 / math.sqrt(HEAD_DIM)

    def score(g, carry):
        q = qs[g].reshape(32, 128).astype(bf16)
        k = keys[pl.ds(g * 8, 8)].reshape(512, 128)
        sc[g] = lax.dot_general(q, k, (((1,), (1,)), ((), ())), preferred_element_type=f32)
        return carry

    lax.fori_loop(0, 16, score, 0, unroll=4)
    col = lax.broadcasted_iota(jnp.int32, (4, 8, 512), 2)
    row = lax.broadcasted_iota(jnp.int32, (4, 8, 512), 1)
    mine = (col // 64) == row
    pos = (col % 64).astype(f32)

    def weigh(g, carry):
        s = sc[g].reshape(4, 8, 512) * root
        here = lengths[pl.ds(pl.multiple_of(g * 8, 8), 8), 0:1]
        keep = jnp.logical_and(mine, pos < here[None])
        s = jnp.where(keep, s, -jnp.inf)
        own = jnp.sum(qs[g] * fs[g][None], axis=-1, keepdims=True) * root
        top = jnp.maximum(jnp.max(s, axis=-1, keepdims=True), own)
        e = jnp.exp(s - top)
        eo = jnp.exp(own - top)
        div = jnp.sum(e, axis=-1, keepdims=True) + eo
        w = (e / div).astype(bf16).reshape(32, 512)
        wo = (eo / div).astype(bf16).astype(f32)
        v = vals[pl.ds(g * 8, 8)].reshape(512, 128)
        o = jnp.dot(w, v, preferred_element_type=f32).reshape(4, 8, 128) + wo * vs[g][None]
        for h in range(4):
            out[g, :, h * 128 : h * 128 + 128] = o[h]
        return carry

    lax.fori_loop(0, 16, weigh, 0, unroll=4)
    att[...] = out[...].reshape(ROWS, 512).astype(bf16)


def place(zh, c, own, part, into):
    for s in range(4):
        t = ((zh + 4 - s) % 4) * 2
        into[t + c] = own[s]
        into[t + 1 - c] = part[s]


def rows_kernel(idx, w, mine, other):
    zl = idx[0]
    for q in range(2):
        to = slice(q * 1024, q * 1024 + 1024)
        for out, z in ((mine, zl), (other, 1 - zl)):
            cols = pl.ds(pl.multiple_of(q * 2048 + z * 1024, 1024), 1024)
            out[:, to] = w[:, cols].astype(bf16)


def halves_kernel(mine, got, e0, e1):
    for z, w in enumerate((mine, got)):
        e0[z] = w[:, :CUT]
        e1[z] = w[:, CUT:]


def out_kernel(*refs):
    idx = refs[0]
    own, three, two = refs[1:5], refs[5], refs[6]
    part = (three[0], three[1], two[...], three[2])
    ya, xa = refs[7:11], refs[11:15]
    keep, send, att, acc0, acc1 = refs[15:20]
    zl, zh, c = idx[0], idx[3], idx[4]
    for s in range(4):
        k = (zh + 4 - s) % 4
        rows = pl.ds(pl.multiple_of(k % 2 * ROWS, ROWS), ROWS)
        att[k // 2 * 2 + c, rows] = own[s][...]
        att[k // 2 * 2 + 1 - c, rows] = part[s]
    nt = (((1,), (1,)), ((), ()))

    def add(a, acc, first):
        def step(t, carry):
            for u in range(2):
                cols = pl.ds(pl.multiple_of(t * 512 + u * 256, 256), 256)
                lhs = jnp.concatenate([r[:, :, :, cols].reshape(-1, 256) for r in a], axis=0)
                rhs = att[first + t][:, u * 256 : u * 256 + 256]
                acc[...] += lax.dot_general(lhs, rhs, nt, preferred_element_type=f32)
            return carry

        return step

    acc0[...] = jnp.zeros((1024, 256), f32)
    acc1[...] = jnp.zeros((1024, 256), f32)
    for a, acc, first, last in ((ya, acc0, 0, CUT), (xa, acc1, CUT, 2048)):
        lax.fori_loop(0, (last - first) // 512, add(a, acc, first // 512), 0)
    here = pl.ds(pl.multiple_of(zl * ROWS, ROWS), ROWS)
    there = pl.ds(pl.multiple_of(ROWS - zl * ROWS, ROWS), ROWS)
    for xs in range(4):
        for ys in range(4):
            i, j = (ys * 4 + xs) * 64, (xs * 4 + ys) * 64
            keep[xs, ys] = acc0[i : i + 64, here] + acc1[j : j + 64, here]
            total = (acc0[i : i + 64, there] + acc1[j : j + 64, there]).astype(bf16)
            send[xs, ys, 0:32] = total[32:]
            send[xs, ys, 32:64] = total[:32]


def add_kernel(keep, got, out):
    for xs in range(4):
        out[xs] = (keep[xs] + got[xs].astype(f32)).astype(bf16)


def final_kernel(*refs):
    idx = refs[0]
    own = [r[...] for r in refs[1:5]]
    part = [refs[5][0], refs[5][1], refs[6][...], refs[5][2]]
    hid, gain, new, normed, pieces, res = refs[7:13]
    zl, x, y = idx[0], idx[1], idx[2]
    place(idx[3], idx[4], own, part, pieces)
    a = lax.broadcasted_iota(jnp.int32, (ROWS, ROWS), 0)
    b = lax.broadcasted_iota(jnp.int32, (ROWS, ROWS), 1)
    eye = jnp.where(a == b, 1.0, 0.0).astype(bf16)
    nt = (((1,), (1,)), ((), ()))

    def step(j, total):
        xs, ys = j // 4, j % 4
        for zs in range(2):
            dp = ((zl ^ zs) * 4 + (x + 4 - xs) % 4) * 4 + (y + 4 - ys) % 4
            cols = pl.ds(pl.multiple_of(dp * 256, 256), 256)
            chunk = jnp.concatenate(
                [pieces[t, xs, ys, zs * 32 : zs * 32 + 32] for t in range(8)], axis=0
            )
            mixed = lax.dot_general(eye, chunk, nt, preferred_element_type=f32)
            r = hid[:, cols].astype(f32) + mixed
            total = total + r * r
            res[:, cols] = r
            new[:, cols] = r.astype(bf16)
        return total

    total = lax.fori_loop(0, 16, step, jnp.zeros((ROWS, 256), f32), unroll=2)
    scale = lax.rsqrt(jnp.sum(total, axis=-1, keepdims=True) / D + epsilon)

    def finish(j, carry):
        cols = pl.ds(pl.multiple_of(j * 1024, 1024), 1024)
        normed[:, cols] = (res[:, cols] * scale * gain[:, cols]).astype(bf16)
        return carry

    lax.fori_loop(0, 8, finish, 0)


def call(kernel, outs, *args, scratch=(), limit=16, near=True):
    def scalars(a):
        return a.dtype == jnp.int32 and a.ndim == 1

    return pl.pallas_call(
        kernel,
        out_shape=outs,
        in_specs=[SM if scalars(a) else VM for a in args],
        out_specs=jax.tree.map(lambda _: VM, outs),
        scratch_shapes=[pltpu.VMEM(*x) for x in scratch],
        compiler_params=pltpu.CompilerParams(vmem_limit_bytes=limit << 20),
    )(*[a if scalars(a) or not near else pltpu.with_memory_space_constraint(a, pltpu.VMEM) for a in args])


def fetch_kernel(keys, vals, keys_out, vals_out, sems):
    first = pltpu.make_async_copy(keys, keys_out, sems.at[0])
    second = pltpu.make_async_copy(vals, vals_out, sems.at[1])
    first.start()
    second.start()
    first.wait()
    second.wait()


def fetch(keys, vals):
    cache = pltpu.VMEM((ROWS, 64, HEAD_DIM), bf16)
    hbm = pl.BlockSpec(memory_space=pl.ANY)
    return pl.pallas_call(
        fetch_kernel,
        out_shape=[cache, cache],
        in_specs=[hbm, hbm],
        out_specs=[VM, VM],
        scratch_shapes=[pltpu.SemaphoreType.DMA((2,))],
        compiler_params=pltpu.CompilerParams(vmem_limit_bytes=1 << 20),
        name="fetch",
    )(keys, vals)


def body(hidden, q_weight, k_weight, v_weight, o_weight, input_gain, post_gain, key_cache, value_cache, lengths):
    zl, x, y, zh, c = (lax.axis_index(a) for a in ("zl", "x", "y", "zh", "c"))
    idx = idx0 = jnp.stack([zl, x, y, zh, c]).astype(jnp.int32)
    sds, vm = jax.ShapeDtypeStruct, pltpu.VMEM

    def move(value, axis, step):
        return shift(value, axis, 2 if axis in ("zl", "c") else 4, step)

    cut = call(cut_kernel, vm((8, 32, 768), bf16), q_weight, k_weight, v_weight, near=False, limit=60)
    block = lax.all_to_all(cut, ("zh", "c"), split_axis=0, concat_axis=0, tiled=True)
    block = block.reshape(256, 768)
    across = move(block, "zl", 1)
    w1, w3 = move(block, "x", 1), move(block, "x", 3)
    v1, v3 = move(across, "x", 1), move(across, "x", 3)
    wa, wb = move(w1[:128], "x", 1), move(w3[128:], "x", 3)
    va, vb = move(v1[:128], "x", 1), move(v3[128:], "x", 3)

    half = pltpu.HBM((64, 2048), bf16)
    h0, *hs = call(
        norm_kernel,
        [pltpu.HBM((2, 64, 2048), bf16), half, half, half],
        idx, hidden, input_gain.reshape(1, D),
        scratch=[((ROWS, 128), f32)],
    )
    hown = [move(hs[s - 1], "y", s) for s in (1, 2, 3)]
    hpart = move(jnp.stack(hown), "c", 1)

    acc = call(first_kernel, vm((512, 768), f32), h0, *hown, hpart, block, w1, w3, across, limit=8)
    full, short = vm((ROWS, 768), f32), vm((ROWS, 768), bf16)
    parts = call(second_kernel, [full, short, short, short], h0, *hown, hpart, v1, v3, wa, wb, va, vb, acc, limit=8)
    back = [move(parts[s], "y", -s) for s in (1, 2, 3)]

    index_row = jnp.arange(64, dtype=f32)
    frequency = jnp.exp(-math.log(rope_base) * index_row / 64)
    angle = lengths.astype(f32)[:, None] * frequency[None, :]
    cos, sin = jnp.cos(angle), jnp.sin(angle)
    head = sds((ROWS, 128), bf16)
    attended, fresh, newv = call(
        attend_kernel,
        [vm((ROWS, 512), bf16), head, head],
        idx, parts[0], *back,
        jnp.concatenate([cos, cos], axis=1),
        jnp.concatenate([-sin, sin], axis=1),
        jnp.broadcast_to(lengths.astype(f32)[:, None], (ROWS, 128)),
        *fetch(key_cache.reshape(ROWS, 64, 128), value_cache.reshape(ROWS, 64, 128)),
        scratch=[
            ((ROWS, 768), f32),
            ((16, 4, 8, 128), f32),
            ((16, 8, 128), f32),
            ((16, 8, 128), f32),
            ((16, 32, 512), f32),
            ((16, 8, 512), f32),
        ],
    )

    shard = vm((32, 2048), bf16)
    mine_o, other_o = call(rows_kernel, [shard] * 2, idx0, o_weight, near=False, limit=60)
    e0, e1 = call(
        halves_kernel,
        [vm((2, 32, CUT), bf16), vm((2, 32, 2048 - CUT), bf16)],
        mine_o, move(other_o, "zl", 1),
    )
    around = [e0] + [move(e0, "x", s) for s in (1, 2, 3)]
    s0 = jnp.stack(around)
    s1 = jnp.stack([e1] + [move(e1, "y", s) for s in (1, 2, 3)])
    rows_y = [s0] + [move(s0, "y", s) for s in (1, 2, 3)]
    rows_x = [s1] + [move(s1, "x", s) for s in (1, 2, 3)]

    def deal_heads(value, turn):
        pairs = []
        for z in range(8):
            to = z // 2 % 2 * 4 + (z % 2 + z // 4 * 2 + turn) % 4
            pairs.append((z % 2 * 4 + z // 2, to))
        return lax.ppermute(value, ("zl", "zh"), pairs)

    def spread(own):
        first = move(jnp.stack([own[0], own[1], own[3]]), "c", 1)
        return own + [first, move(own[2], "c", 1)]

    heads = spread([deal_heads(attended, s) for s in range(4)])
    tile = (4, 4, 64, ROWS)
    keep, send = call(
        out_kernel,
        [vm(tile, f32), vm(tile, bf16)],
        idx, *heads, *rows_y, *rows_x,
        scratch=[((4, 256, 512), bf16), ((1024, 256), f32), ((1024, 256), f32)],
    )
    mixed_t = call(add_kernel, vm(tile, bf16), keep, move(send, "zl", 1), limit=4)
    pieces = spread([mixed_t] + [move(mixed_t, "zh", s) for s in (1, 2, 3)])
    new_hidden, normed = call(
        final_kernel,
        [sds((ROWS, D), bf16)] * 2,
        idx, *pieces, hidden, post_gain.reshape(1, D),
        scratch=[((8, 4, 4, 64, ROWS), bf16), ((ROWS, D), f32)],
    )
    return (new_hidden, normed, fresh.reshape(ROWS, 1, 128), newv.reshape(ROWS, 1, 128))


def solution(mesh):
    torus = Mesh(mesh.devices.reshape(2, 4, 4, 4, 2), ("zl", "x", "y", "zh", "c"))
    dp, tensor = ("zl", "x", "y"), ("zh", "c")
    in_specs = (
        P(dp, None),
        P(dp + tensor, None),
        P(dp + tensor, None),
        P(dp + tensor, None),
        P(dp + tensor, None),
        P(),
        P(),
        P(dp, None, tensor, None),
        P(dp, None, tensor, None),
        P(dp),
    )
    out_specs = (P(dp, None), P(dp, None), P(dp, tensor, None), P(dp, tensor, None))
    return jax.shard_map(body, mesh=torus, in_specs=in_specs, out_specs=out_specs, check_vma=False)
```

time: 505 us -> 192 us (0.38)
  the two profiles are of different devices: /device:TPU:2 before, /device:TPU:73 now
where the time goes in v1:
time: 192 us; the launch traced here: 191 us
  waiting for transfers between devices  89.8 us (47%)
  starting transfers between devices  72.6 us (38%)
  Pallas kernels  22.8 us (12%)
  local copies, waits for them, and re-layouts  3.69 us (2%)
    ppermute x37, waiting for transfers between devices, shift(): lax.ppermute(value, axis, [(i, (i + step) % size) for i in range(size)])  80.2 us
    ppermute x37, starting transfers between devices, shift(): lax.ppermute(value, axis, [(i, (i + step) % size) for i in range(size)])  54 us
    pallas_call x10, Pallas kernels, call(): pl.pallas_call(kernel, out_shape=outs, in_specs=[SM if scalars(a) else VM...  22.5 us
    ppermute x4, starting transfers between devices, deal_heads(): return lax.ppermute(value, ('zl', 'zh'), pairs)  10.2 us
    all_to_all x1, starting transfers between devices, body(): lax.all_to_all(cut, ('zh', 'c'), split_axis=0, concat_axis=0, tiled=True)  8.4 us
    ppermute x4, waiting for transfers between devices, deal_heads(): return lax.ppermute(value, ('zl', 'zh'), pairs)  7.84 us
  transfers between devices with their start and end apart: 42, of which 19 were waited for; matrix products, arithmetic and copies ran while one was open for 1% of the time, Pallas kernels for 7%

profile of v1, /device:TPU:73, one launch (start us, length us, event | category | flops | bytes accessed | tf_op | source)
XLA Modules:
  0.0 191.5 jit_solution(3776704437902760594)
XLA Ops:
  2.6 8.4 %all-to-all-start = ((bf16[8,32,768]{2,1,0:T(8,128)(2,1)}), bf16[8,32,768]{2,1,0:T(8,128)(2,1)S(1)}, u32[]{:S(2)}, u32[]{:S(2)}) async-start(bf16[8,32,768]{2,1,0:T(8,128)(2,1)} %shard_map.130), calls=%async_computation | async-start | bytes 786432 | tf_op jit(solution)/shard_map/all_to_all | solution.py:305
  13.4 3.5 %shard_map.129 = (bf16[2,64,2048]{2,1,0:T(8,128)(2,1)}, bf16[64,2048]{1,0:T(8,128)(2,1)}, bf16[64,2048]{1,0:T(8,128)(2,1)}, bf16[64,2048]{1,0:T(8,128)(2,1)}) custom-call(s32[5]{0:T(128)S(1)} %stack.89.idx.refs_0_, bf16[128,8192]{1,0:T(8,128)(2,1)S(1)} %copy-done, f32[1,8192]{1,0:T(1,128)S(1)} %bitcast.46), custom_call_target="tpu_custom_call" | custom-call | tf_op jit(solution)/shard_map/pallas_call | solution.py:263
  24.6 2.6 %collective-permute-done.1.hb = bf16[64,2048]{1,0:T(8,128)(2,1)S(1)} collective-permute-done((bf16[64,2048]{1,0:T(8,128)(2,1)}, bf16[64,2048]{1,0:T(8,128)(2,1)S(1)}, u32[]{:S(2)}, u32[]{:S(2)}) %collective-permute-start.1) | collective-permute-done | bytes 262176 | tf_op jit(solution)/shard_map/ppermute | solution.py:27
  27.2 5.3 %collective-permute-done.2.hc = bf16[64,2048]{1,0:T(8,128)(2,1)S(1)} collective-permute-done((bf16[64,2048]{1,0:T(8,128)(2,1)}, bf16[64,2048]{1,0:T(8,128)(2,1)S(1)}, u32[]{:S(2)}, u32[]{:S(2)}) %collective-permute-start.2) | collective-permute-done | bytes 262176 | tf_op jit(solution)/shard_map/ppermute | solution.py:27
  37.2 2.5 %collective-permute-start.6 = (bf16[256,768]{1,0:T(8,128)(2,1)}, bf16[256,768]{1,0:T(8,128)(2,1)S(1)}, u32[]{:S(2)}, u32[]{:S(2)}) collective-permute-start(bf16[256,768]{1,0:T(8,128)(2,1)} %collective-permute-done.4.v0), channel_id=1, source_target_pairs={{0,96},{32,0},{64,32},{96,64},{1,97},{33,1},{65,33},{97,65},{2,98}... | collective-permute-start | bytes 1179656 | tf_op jit(solution)/shard_map/ppermute | solution.py:27
  40.8 4.7 %collective-permute-done.9.w3 = bf16[256,768]{1,0:T(8,128)(2,1)S(1)} collective-permute-done((bf16[256,768]{1,0:T(8,128)(2,1)S(1)}, bf16[256,768]{1,0:T(8,128)(2,1)S(1)}, u32[]{:S(2)}, u32[]{:S(2)}) %collective-permute-start.9) | collective-permute-done | bytes 393248 | tf_op jit(solution)/shard_map/ppermute | solution.py:27
  50.7 6.4 %collective-permute-done.5.v1 = bf16[256,768]{1,0:T(8,128)(2,1)S(1)} collective-permute-done((bf16[256,768]{1,0:T(8,128)(2,1)}, bf16[256,768]{1,0:T(8,128)(2,1)S(1)}, u32[]{:S(2)}, u32[]{:S(2)}) %collective-permute-start.5) | collective-permute-done | bytes 393248 | tf_op jit(solution)/shard_map/ppermute | solution.py:27
  57.2 2.8 %collective-permute-start.12 = (bf16[128,768]{1,0:T(8,128)(2,1)S(1)}, bf16[128,768]{1,0:T(8,128)(2,1)S(1)}, u32[]{:S(2)}, u32[]{:S(2)}) collective-permute-start(bf16[128,768]{1,0:T(8,128)(2,1)S(1)} %slice.19), channel_id=1, source_target_pairs={{0,96},{32,0},{64,32},{96,64},{1,97},{33,1},{65,33},{97,65},{2,98}... | collective-permute-start | bytes 589832 | tf_op jit(solution)/shard_map/ppermute | solution.py:27
  60.1 2.6 %collective-permute-start.24 = (bf16[2,32,1024]{2,1,0:T(8,128)(2,1)S(1)}, bf16[2,32,1024]{2,1,0:T(8,128)(2,1)S(1)}, u32[]{:S(2)}, u32[]{:S(2)}) collective-permute-start(bf16[2,32,1024]{2,1,0:T(8,128)(2,1)S(1)} %get-tuple-element.38), channel_id=1, source_target_pairs={{0,64},{32,96},{64,0},{96,32},{1,65},{33,97},{65,1},{97,33},{2,66}... | collective-permute-start | bytes 393224 | tf_op jit(solution)/shard_map/ppermute | solution.py:27
  76.2 14.0 %collective-permute-done.29 = bf16[2,32,1024]{2,1,0:T(8,128)(2,1)S(1)} collective-permute-done((bf16[2,32,1024]{2,1,0:T(8,128)(2,1)S(1)}, bf16[2,32,1024]{2,1,0:T(8,128)(2,1)S(1)}, u32[]{:S(2)}, u32[]{:S(2)}) %collective-permute-start.29) | collective-permute-done | bytes 131104 | tf_op jit(solution)/shard_map/ppermute | solution.py:27
  91.4 2.8 %collective-permute-start.31 = (bf16[2,32,1024]{2,1,0:T(8,128)(2,1)S(1)}, bf16[2,32,1024]{2,1,0:T(8,128)(2,1)S(1)}, u32[]{:S(2)}, u32[]{:S(2)}) collective-permute-start(bf16[2,32,1024]{2,1,0:T(8,128)(2,1)S(1)} %get-tuple-element.39), channel_id=1, source_target_pairs={{0,24},{8,0},{16,8},{24,16},{1,25},{9,1},{17,9},{25,17},{2,26},{10... | collective-permute-start | bytes 393224 | tf_op jit(solution)/shard_map/ppermute | solution.py:27
  97.1 4.0 %shard_map.133 = (bf16[128,512]{1,0:T(8,128)(2,1)S(1)}, bf16[128,128]{1,0:T(8,128)(2,1)}, bf16[128,128]{1,0:T(8,128)(2,1)}) custom-call(s32[5]{0:T(128)S(1)} %copy-done.8, f32[128,768]{1,0:T(8,128)S(1)} %get-tuple-element.29.p0, bf16[128,768]{1,0:T(8,128)(2,1)S(1)} %collective-permute-done.13.r1, bf16[128,768]{1,0:T(8,128)(2,1)S(1)} %collective-permute-done.14.r2, ...), custom_call_target="tpu_custom_call" | custom-call | tf_op jit(solution)/shard_map/pallas_call | solution.py:263
  103.1 4.7 %collective-permute-start.19 = (bf16[128,512]{1,0:T(8,128)(2,1)S(1)}, bf16[128,512]{1,0:T(8,128)(2,1)S(1)}, u32[]{:S(2)}, u32[]{:S(2)}) collective-permute-start(bf16[128,512]{1,0:T(8,128)(2,1)S(1)} %get-tuple-element.35), channel_id=1, source_target_pairs={{0,6},{128,0},{2,134},{130,128},{4,2},{132,4},{6,130},{134,132},{1... | collective-permute-start | bytes 393224 | tf_op jit(solution)/shard_map/ppermute | solution.py:369
  113.7 10.9 %collective-permute-start.20 = (bf16[3,128,512]{2,1,0:T(8,128)(2,1)S(1)}, bf16[3,128,512]{2,1,0:T(8,128)(2,1)S(1)}, u32[]{:S(2)}, u32[]{:S(2)}) collective-permute-start(bf16[3,128,512]{2,1,0:T(8,128)(2,1)S(1)} %pad_maximum_fusion.4), channel_id=1, source_target_pairs={{0,1},{1,0},{2,3},{3,2},{4,5},{5,4},{6,7},{7,6},{8,9},{9,8},{10,11... | collective-permute-start | bytes 1179656 | tf_op jit(solution)/shard_map/ppermute | solution.py:27
  124.6 3.5 %collective-permute-start.18 = (bf16[128,512]{1,0:T(8,128)(2,1)S(1)}, bf16[128,512]{1,0:T(8,128)(2,1)S(1)}, u32[]{:S(2)}, u32[]{:S(2)}) collective-permute-start(bf16[128,512]{1,0:T(8,128)(2,1)S(1)} %get-tuple-element.35), channel_id=1, source_target_pairs={{0,4},{128,6},{2,132},{130,134},{4,0},{132,2},{6,128},{134,130},{1... | collective-permute-start | bytes 393224 | tf_op jit(solution)/shard_map/ppermute | solution.py:369
  128.1 7.3 %collective-permute-done.18.refs_3_ = bf16[128,512]{1,0:T(8,128)(2,1)S(1)} collective-permute-done((bf16[128,512]{1,0:T(8,128)(2,1)S(1)}, bf16[128,512]{1,0:T(8,128)(2,1)S(1)}, u32[]{:S(2)}, u32[]{:S(2)}) %collective-permute-start.18) | collective-permute-done | bytes 131104 | tf_op jit(solution)/shard_map/ppermute | solution.py:369
  137.3 2.8 %shard_map.136 = (f32[4,4,64,128]{3,2,1,0:T(8,128)S(1)}, bf16[4,4,64,128]{3,2,1,0:T(8,128)(2,1)S(1)}) custom-call(s32[5]{0:T(128)S(1)} %copy-done.8, bf16[128,512]{1,0:T(8,128)(2,1)S(1)} %collective-permute-done.16.refs_1_, bf16[128,512]{1,0:T(8,128)(2,1)S(1)} %collective-permute-done.17.refs_2_, bf16[128,512]{1,0:T(8,128)(2,1)S(1)} %collective-permute-done.18.refs_3_, ...), custom_call_target="tpu_custom_call" | custom-call | tf_op jit(solution)/shard_map/pallas_call | solution.py:263
  140.2 7.5 %collective-permute-done.35.got = bf16[4,4,64,128]{3,2,1,0:T(8,128)(2,1)S(1)} collective-permute-done((bf16[4,4,64,128]{3,2,1,0:T(8,128)(2,1)S(1)}, bf16[4,4,64,128]{3,2,1,0:T(8,128)(2,1)S(1)}, u32[]{:S(2)}, u32[]{:S(2)}) %collective-permute-start.35) | collective-permute-done | bytes 262176 | tf_op jit(solution)/shard_map/ppermute | solution.py:27
  147.8 3.7 %collective-permute-start.36 = (bf16[4,4,64,128]{3,2,1,0:T(8,128)(2,1)S(1)}, bf16[4,4,64,128]{3,2,1,0:T(8,128)(2,1)S(1)}, u32[]{:S(2)}, u32[]{:S(2)}) collective-permute-start(bf16[4,4,64,128]{3,2,1,0:T(8,128)(2,1)S(1)} %shard_map.137.refs_1_), channel_id=1, source_target_pairs={{0,2},{2,4},{4,6},{6,0},{1,3},{3,5},{5,7},{7,1},{8,10},{10,12},{12... | collective-permute-start | bytes 786440 | tf_op jit(solution)/shard_map/ppermute | solution.py:27
  151.5 7.1 %collective-permute-done.36.refs_2_ = bf16[4,4,64,128]{3,2,1,0:T(8,128)(2,1)S(1)} collective-permute-done((bf16[4,4,64,128]{3,2,1,0:T(8,128)(2,1)S(1)}, bf16[4,4,64,128]{3,2,1,0:T(8,128)(2,1)S(1)}, u32[]{:S(2)}, u32[]{:S(2)}) %collective-permute-start.36) | collective-permute-done | bytes 262176 | tf_op jit(solution)/shard_map/ppermute | solution.py:27
  158.6 8.2 %collective-permute-done.38.refs_4_ = bf16[4,4,64,128]{3,2,1,0:T(8,128)(2,1)S(1)} collective-permute-done((bf16[4,4,64,128]{3,2,1,0:T(8,128)(2,1)S(1)}, bf16[4,4,64,128]{3,2,1,0:T(8,128)(2,1)S(1)}, u32[]{:S(2)}, u32[]{:S(2)}) %collective-permute-start.38) | collective-permute-done | bytes 262176 | tf_op jit(solution)/shard_map/ppermute | solution.py:27
  167.5 2.5 %collective-permute-start.37 = (bf16[4,4,64,128]{3,2,1,0:T(8,128)(2,1)S(1)}, bf16[4,4,64,128]{3,2,1,0:T(8,128)(2,1)S(1)}, u32[]{:S(2)}, u32[]{:S(2)}) collective-permute-start(bf16[4,4,64,128]{3,2,1,0:T(8,128)(2,1)S(1)} %shard_map.137.refs_1_), channel_id=1, source_target_pairs={{0,4},{2,6},{4,0},{6,2},{1,5},{3,7},{5,1},{7,3},{8,12},{10,14},{12... | collective-permute-start | bytes 786440 | tf_op jit(solution)/shard_map/ppermute | solution.py:27
  170.1 14.4 %collective-permute-done.37.refs_3_ = bf16[4,4,64,128]{3,2,1,0:T(8,128)(2,1)S(1)} collective-permute-done((bf16[4,4,64,128]{3,2,1,0:T(8,128)(2,1)S(1)}, bf16[4,4,64,128]{3,2,1,0:T(8,128)(2,1)S(1)}, u32[]{:S(2)}, u32[]{:S(2)}) %collective-permute-start.37) | collective-permute-done | bytes 262176 | tf_op jit(solution)/shard_map/ppermute | solution.py:27
  186.1 5.4 %shard_map.138 = (bf16[128,8192]{1,0:T(8,128)(2,1)}, bf16[128,8192]{1,0:T(8,128)(2,1)}) custom-call(s32[5]{0:T(128)S(1)} %copy-done.8, bf16[4,4,64,128]{3,2,1,0:T(8,128)(2,1)S(1)} %shard_map.137.refs_1_, bf16[4,4,64,128]{3,2,1,0:T(8,128)(2,1)S(1)} %collective-permute-done.36.refs_2_, bf16[4,4,64,128]{3,2,1,0:T(8,128)(2,1)S(1)} %collective-permute-done.37.refs_3_, ...), custom_call_target="tpu_custom_call" | custom-call | tf_op jit(solution)/shard_map/pallas_call | solution.py:263
  (106 shorter events, 53.0 us)
Async XLA Ops:
  2.6 20.2 %all-to-all-start = ((bf16[8,32,768]{2,1,0:T(8,128)(2,1)}), bf16[8,32,768]{2,1,0:T(8,128)(2,1)S(1)}, u32[]{:S(2)}, u32[]{:S(2)}) async-start(bf16[8,32,768]{2,1,0:T(8,128)(2,1)} %shard_map.130), calls=%async_computation | async-start | bytes 786432 | tf_op jit(solution)/shard_map/all_to_all | solution.py:305
  19.0 13.5 %collective-permute-start.2 = (bf16[64,2048]{1,0:T(8,128)(2,1)}, bf16[64,2048]{1,0:T(8,128)(2,1)S(1)}, u32[]{:S(2)}, u32[]{:S(2)}) collective-permute-start(bf16[64,2048]{1,0:T(8,128)(2,1)} %get-tuple-element.28), channel_id=1, source_target_pairs={{0,24},{8,0},{16,8},{24,16},{1,25},{9,1},{17,9},{25,17},{2,26},{10... | collective-permute-start | bytes 786440 | tf_op jit(solution)/shard_map/ppermute | solution.py:27
  22.8 14.3 %collective-permute-start.4 = (bf16[256,768]{1,0:T(8,128)(2,1)S(1)}, bf16[256,768]{1,0:T(8,128)(2,1)}, u32[]{:S(2)}, u32[]{:S(2)}) collective-permute-start(bf16[256,768]{1,0:T(8,128)(2,1)S(1)} %bitcast.35), channel_id=1, source_target_pairs={{0,128},{128,0},{1,129},{129,1},{2,130},{130,2},{3,131},{131,3},{4... | collective-permute-start | bytes 1179656 | tf_op jit(solution)/shard_map/ppermute | solution.py:27
  33.5 26.5 %collective-permute-start.3 = (bf16[3,64,2048]{2,1,0:T(8,128)(2,1)}, bf16[3,64,2048]{2,1,0:T(8,128)(2,1)S(1)}, u32[]{:S(2)}, u32[]{:S(2)}) collective-permute-start(bf16[3,64,2048]{2,1,0:T(8,128)(2,1)} %pad_maximum_fusion), channel_id=1, source_target_pairs={{0,1},{1,0},{2,3},{3,2},{4,5},{5,4},{6,7},{7,6},{8,9},{9,8},{10,11... | collective-permute-start | bytes 2359304 | tf_op jit(solution)/shard_map/ppermute | solution.py:27
  37.0 11.7 %collective-permute-start.7 = (bf16[256,768]{1,0:T(8,128)(2,1)S(1)}, bf16[256,768]{1,0:T(8,128)(2,1)}, u32[]{:S(2)}, u32[]{:S(2)}) collective-permute-start(bf16[256,768]{1,0:T(8,128)(2,1)S(1)} %bitcast.37), channel_id=1, source_target_pairs={{0,32},{32,64},{64,96},{96,0},{1,33},{33,65},{65,97},{97,1},{2,34}... | collective-permute-start | bytes 1179656 | tf_op jit(solution)/shard_map/ppermute | solution.py:27
  37.0 20.0 %collective-permute-start.5 = (bf16[256,768]{1,0:T(8,128)(2,1)}, bf16[256,768]{1,0:T(8,128)(2,1)S(1)}, u32[]{:S(2)}, u32[]{:S(2)}) collective-permute-start(bf16[256,768]{1,0:T(8,128)(2,1)} %collective-permute-done.4.v0), channel_id=1, source_target_pairs={{0,32},{32,64},{64,96},{96,0},{1,33},{33,65},{65,97},{97,1},{2,34}... | collective-permute-start | bytes 1179656 | tf_op jit(solution)/shard_map/ppermute | solution.py:27
  37.2 19.8 %collective-permute-start.6 = (bf16[256,768]{1,0:T(8,128)(2,1)}, bf16[256,768]{1,0:T(8,128)(2,1)S(1)}, u32[]{:S(2)}, u32[]{:S(2)}) collective-permute-start(bf16[256,768]{1,0:T(8,128)(2,1)} %collective-permute-done.4.v0), channel_id=1, source_target_pairs={{0,96},{32,0},{64,32},{96,64},{1,97},{33,1},{65,33},{97,65},{2,98}... | collective-permute-start | bytes 1179656 | tf_op jit(solution)/shard_map/ppermute | solution.py:27
  45.5 11.7 %collective-permute-start.22 = (bf16[32,2048]{1,0:T(8,128)(2,1)S(1)}, bf16[32,2048]{1,0:T(8,128)(2,1)S(1)}, u32[]{:S(2)}, u32[]{:S(2)}) collective-permute-start(bf16[32,2048]{1,0:T(8,128)(2,1)S(1)} %get-tuple-element.37), channel_id=1, source_target_pairs={{0,128},{128,0},{1,129},{129,1},{2,130},{130,2},{3,131},{131,3},{4... | collective-permute-start | bytes 393224 | tf_op jit(solution)/shard_map/ppermute | solution.py:27
  60.0 13.4 %collective-permute-start.23 = (bf16[2,32,1024]{2,1,0:T(8,128)(2,1)S(1)}, bf16[2,32,1024]{2,1,0:T(8,128)(2,1)S(1)}, u32[]{:S(2)}, u32[]{:S(2)}) collective-permute-start(bf16[2,32,1024]{2,1,0:T(8,128)(2,1)S(1)} %get-tuple-element.38), channel_id=1, source_target_pairs={{0,32},{32,64},{64,96},{96,0},{1,33},{33,65},{65,97},{97,1},{2,34}... | collective-permute-start | bytes 393224 | tf_op jit(solution)/shard_map/ppermute | solution.py:27
  60.1 14.3 %collective-permute-start.24 = (bf16[2,32,1024]{2,1,0:T(8,128)(2,1)S(1)}, bf16[2,32,1024]{2,1,0:T(8,128)(2,1)S(1)}, u32[]{:S(2)}, u32[]{:S(2)}) collective-permute-start(bf16[2,32,1024]{2,1,0:T(8,128)(2,1)S(1)} %get-tuple-element.38), channel_id=1, source_target_pairs={{0,64},{32,96},{64,0},{96,32},{1,65},{33,97},{65,1},{97,33},{2,66}... | collective-permute-start | bytes 393224 | tf_op jit(solution)/shard_map/ppermute | solution.py:27
  69.1 22.2 %collective-permute-start.13 = (bf16[128,768]{1,0:T(8,128)(2,1)S(1)}, bf16[128,768]{1,0:T(8,128)(2,1)S(1)}, u32[]{:S(2)}, u32[]{:S(2)}) collective-permute-start(bf16[128,768]{1,0:T(8,128)(2,1)S(1)} %get-tuple-element.30), channel_id=1, source_target_pairs={{0,24},{8,0},{16,8},{24,16},{1,25},{9,1},{17,9},{25,17},{2,26},{10... | collective-permute-start | bytes 589832 | tf_op jit(solution)/shard_map/ppermute | solution.py:27
  69.7 24.4 %collective-permute-start.14 = (bf16[128,768]{1,0:T(8,128)(2,1)S(1)}, bf16[128,768]{1,0:T(8,128)(2,1)S(1)}, u32[]{:S(2)}, u32[]{:S(2)}) collective-permute-start(bf16[128,768]{1,0:T(8,128)(2,1)S(1)} %get-tuple-element.31), channel_id=1, source_target_pairs={{0,16},{8,24},{16,0},{24,8},{1,17},{9,25},{17,1},{25,9},{2,18},{10... | collective-permute-start | bytes 589832 | tf_op jit(solution)/shard_map/ppermute | solution.py:27
  73.4 22.0 %collective-permute-start.15 = (bf16[128,768]{1,0:T(8,128)(2,1)S(1)}, bf16[128,768]{1,0:T(8,128)(2,1)S(1)}, u32[]{:S(2)}, u32[]{:S(2)}) collective-permute-start(bf16[128,768]{1,0:T(8,128)(2,1)S(1)} %get-tuple-element.32), channel_id=1, source_target_pairs={{0,8},{8,16},{16,24},{24,0},{1,9},{9,17},{17,25},{25,1},{2,10},{10... | collective-permute-start | bytes 589832 | tf_op jit(solution)/shard_map/ppermute | solution.py:27
  74.5 28.5 %collective-permute-start.26 = (bf16[4,2,32,1024]{3,2,1,0:T(8,128)(2,1)S(1)}, bf16[4,2,32,1024]{3,2,1,0:T(8,128)(2,1)S(1)}, u32[]{:S(2)}, u32[]{:S(2)}) collective-permute-start(bf16[4,2,32,1024]{3,2,1,0:T(8,128)(2,1)S(1)} %pad_maximum_fusion.2.refs_7_), channel_id=1, source_target_pairs={{0,8},{8,16},{16,24},{24,0},{1,9},{9,17},{17,25},{25,1},{2,10},{10... | collective-permute-start | bytes 1572872 | tf_op jit(solution)/shard_map/ppermute | solution.py:27
  75.3 14.8 %collective-permute-start.29 = (bf16[2,32,1024]{2,1,0:T(8,128)(2,1)S(1)}, bf16[2,32,1024]{2,1,0:T(8,128)(2,1)S(1)}, u32[]{:S(2)}, u32[]{:S(2)}) collective-permute-start(bf16[2,32,1024]{2,1,0:T(8,128)(2,1)S(1)} %get-tuple-element.39), channel_id=1, source_target_pairs={{0,8},{8,16},{16,24},{24,0},{1,9},{9,17},{17,25},{25,1},{2,10},{10... | collective-permute-start | bytes 393224 | tf_op jit(solution)/shard_map/ppermute | solution.py:27
  94.2 19.5 %collective-permute-start.27 = (bf16[4,2,32,1024]{3,2,1,0:T(8,128)(2,1)S(1)}, bf16[4,2,32,1024]{3,2,1,0:T(8,128)(2,1)S(1)}, u32[]{:S(2)}, u32[]{:S(2)}) collective-permute-start(bf16[4,2,32,1024]{3,2,1,0:T(8,128)(2,1)S(1)} %pad_maximum_fusion.2.refs_7_), channel_id=1, source_target_pairs={{0,16},{8,24},{16,0},{24,8},{1,17},{9,25},{17,1},{25,9},{2,18},{10... | collective-permute-start | bytes 1572872 | tf_op jit(solution)/shard_map/ppermute | solution.py:27
  95.4 29.2 %collective-permute-start.28 = (bf16[4,2,32,1024]{3,2,1,0:T(8,128)(2,1)S(1)}, bf16[4,2,32,1024]{3,2,1,0:T(8,128)(2,1)S(1)}, u32[]{:S(2)}, u32[]{:S(2)}) collective-permute-start(bf16[4,2,32,1024]{3,2,1,0:T(8,128)(2,1)S(1)} %pad_maximum_fusion.2.refs_7_), channel_id=1, source_target_pairs={{0,24},{8,0},{16,8},{24,16},{1,25},{9,1},{17,9},{25,17},{2,26},{10... | collective-permute-start | bytes 1572872 | tf_op jit(solution)/shard_map/ppermute | solution.py:27
  108.4 27.9 %collective-permute-start.32 = (bf16[4,2,32,1024]{3,2,1,0:T(8,128)(2,1)S(1)}, bf16[4,2,32,1024]{3,2,1,0:T(8,128)(2,1)S(1)}, u32[]{:S(2)}, u32[]{:S(2)}) collective-permute-start(bf16[4,2,32,1024]{3,2,1,0:T(8,128)(2,1)S(1)} %pad_maximum_fusion.3.refs_11_), channel_id=1, source_target_pairs={{0,32},{32,64},{64,96},{96,0},{1,33},{33,65},{65,97},{97,1},{2,34}... | collective-permute-start | bytes 1572872 | tf_op jit(solution)/shard_map/ppermute | solution.py:27
  110.5 25.8 %collective-permute-start.33 = (bf16[4,2,32,1024]{3,2,1,0:T(8,128)(2,1)S(1)}, bf16[4,2,32,1024]{3,2,1,0:T(8,128)(2,1)S(1)}, u32[]{:S(2)}, u32[]{:S(2)}) collective-permute-start(bf16[4,2,32,1024]{3,2,1,0:T(8,128)(2,1)S(1)} %pad_maximum_fusion.3.refs_11_), channel_id=1, source_target_pairs={{0,64},{32,96},{64,0},{96,32},{1,65},{33,97},{65,1},{97,33},{2,66}... | collective-permute-start | bytes 1572872 | tf_op jit(solution)/shard_map/ppermute | solution.py:27
  111.5 24.8 %collective-permute-start.34 = (bf16[4,2,32,1024]{3,2,1,0:T(8,128)(2,1)S(1)}, bf16[4,2,32,1024]{3,2,1,0:T(8,128)(2,1)S(1)}, u32[]{:S(2)}, u32[]{:S(2)}) collective-permute-start(bf16[4,2,32,1024]{3,2,1,0:T(8,128)(2,1)S(1)} %pad_maximum_fusion.3.refs_11_), channel_id=1, source_target_pairs={{0,96},{32,0},{64,32},{96,64},{1,97},{33,1},{65,33},{97,65},{2,98}... | collective-permute-start | bytes 1572872 | tf_op jit(solution)/shard_map/ppermute | solution.py:27
  113.7 23.7 %collective-permute-start.20 = (bf16[3,128,512]{2,1,0:T(8,128)(2,1)S(1)}, bf16[3,128,512]{2,1,0:T(8,128)(2,1)S(1)}, u32[]{:S(2)}, u32[]{:S(2)}) collective-permute-start(bf16[3,128,512]{2,1,0:T(8,128)(2,1)S(1)} %pad_maximum_fusion.4), channel_id=1, source_target_pairs={{0,1},{1,0},{2,3},{3,2},{4,5},{5,4},{6,7},{7,6},{8,9},{9,8},{10,11... | collective-permute-start | bytes 1179656 | tf_op jit(solution)/shard_map/ppermute | solution.py:27
  151.5 15.4 %collective-permute-start.38 = (bf16[4,4,64,128]{3,2,1,0:T(8,128)(2,1)S(1)}, bf16[4,4,64,128]{3,2,1,0:T(8,128)(2,1)S(1)}, u32[]{:S(2)}, u32[]{:S(2)}) collective-permute-start(bf16[4,4,64,128]{3,2,1,0:T(8,128)(2,1)S(1)} %shard_map.137.refs_1_), channel_id=1, source_target_pairs={{0,6},{2,0},{4,2},{6,4},{1,7},{3,1},{5,3},{7,5},{8,14},{10,8},{12,... | collective-permute-start | bytes 786440 | tf_op jit(solution)/shard_map/ppermute | solution.py:27
  166.9 19.2 %collective-permute-start.39 = (bf16[3,4,4,64,128]{4,3,2,1,0:T(8,128)(2,1)S(1)}, bf16[3,4,4,64,128]{4,3,2,1,0:T(8,128)(2,1)S(1)}, u32[]{:S(2)}, u32[]{:S(2)}) collective-permute-start(bf16[3,4,4,64,128]{4,3,2,1,0:T(8,128)(2,1)S(1)} %pad_maximum_fusion.1), channel_id=1, source_target_pairs={{0,1},{1,0},{2,3},{3,2},{4,5},{5,4},{6,7},{7,6},{8,9},{9,8},{10,11... | collective-permute-start | bytes 2359304 | tf_op jit(solution)/shard_map/ppermute | solution.py:27
  167.5 17.0 %collective-permute-start.37 = (bf16[4,4,64,128]{3,2,1,0:T(8,128)(2,1)S(1)}, bf16[4,4,64,128]{3,2,1,0:T(8,128)(2,1)S(1)}, u32[]{:S(2)}, u32[]{:S(2)}) collective-permute-start(bf16[4,4,64,128]{3,2,1,0:T(8,128)(2,1)S(1)} %shard_map.137.refs_1_), channel_id=1, source_target_pairs={{0,4},{2,6},{4,0},{6,2},{1,5},{3,7},{5,1},{7,3},{8,12},{10,14},{12... | collective-permute-start | bytes 786440 | tf_op jit(solution)/shard_map/ppermute | solution.py:27
  (28 other events, 397.5 us)

commit v2 on v1

--- a/solution.py
+++ b/solution.py
@@ -151,13 +151,6 @@
     att[...] = out[...].reshape(ROWS, 512).astype(bf16)
 
 
-def place(zh, c, own, part, into):
-    for s in range(4):
-        t = ((zh + 4 - s) % 4) * 2
-        into[t + c] = own[s]
-        into[t + 1 - c] = part[s]
-
-
 def rows_kernel(idx, w, mine, other):
     zl = idx[0]
     for q in range(2):
@@ -213,18 +206,23 @@
             send[xs, ys, 32:64] = total[:32]
 
 
-def add_kernel(keep, got, out):
-    for xs in range(4):
-        out[xs] = (keep[xs] + got[xs].astype(f32)).astype(bf16)
+def add_kernel(keep, got, low, up):
+    for xs in range(2):
+        low[xs] = (keep[xs] + got[xs].astype(f32)).astype(bf16)
+        up[xs] = (keep[xs + 2] + got[xs + 2].astype(f32)).astype(bf16)
 
 
 def final_kernel(*refs):
     idx = refs[0]
-    own = [r[...] for r in refs[1:5]]
-    part = [refs[5][0], refs[5][1], refs[6][...], refs[5][2]]
-    hid, gain, new, normed, pieces, res = refs[7:13]
-    zl, x, y = idx[0], idx[1], idx[2]
-    place(idx[3], idx[4], own, part, pieces)
+    own = refs[1:9]
+    part = [refs[9][i] for i in range(4)] + [refs[10][i] for i in range(2)] + [refs[11][...], refs[12][...]]
+    hid, gain, new, normed, pieces, res = refs[13:19]
+    zl, x, y, zh, c = (idx[i] for i in range(5))
+    where = ((0, 0), (0, 1), (1, 0), (3, 1), (1, 1), (3, 0), (2, 0), (2, 1))
+    for i, (s, h) in enumerate(where):
+        t = ((zh + 4 - s) % 4) * 2
+        pieces[t + c, 2 * h : 2 * h + 2] = own[i][...]
+        pieces[t + 1 - c, 2 * h : 2 * h + 2] = part[i]
     a = lax.broadcasted_iota(jnp.int32, (ROWS, ROWS), 0)
     b = lax.broadcasted_iota(jnp.int32, (ROWS, ROWS), 1)
     eye = jnp.where(a == b, 1.0, 0.0).astype(bf16)
@@ -380,8 +378,14 @@
         idx, *heads, *rows_y, *rows_x,
         scratch=[((4, 256, 512), bf16), ((1024, 256), f32), ((1024, 256), f32)],
     )
-    mixed_t = call(add_kernel, vm(tile, bf16), keep, move(send, "zl", 1), limit=4)
-    pieces = spread([mixed_t] + [move(mixed_t, "zh", s) for s in (1, 2, 3)])
+    half_tile = vm((2, 4, 64, ROWS), bf16)
+    low, up = call(add_kernel, [half_tile] * 2, keep, move(send, "zl", 1), limit=4)
+    a1, a3 = move(low, "zh", 1), move(up, "zh", 3)
+    b1, b3 = move(up, "zh", 1), move(low, "zh", 3)
+    f1, f3 = move(a1, "zh", 1), move(a3, "zh", 3)
+    pieces = [low, up, a1, a3, b1, b3, f1, f3]
+    pieces += [move(jnp.stack([low, up, a1, a3]), "c", 1), move(jnp.stack([b1, b3]), "c", 1)]
+    pieces += [move(f1, "c", 1), move(f3, "c", 1)]
     new_hidden, normed = call(
         final_kernel,
         [sds((ROWS, D), bf16)] * 2,

time: 192 us -> 192 us (level)
  the two profiles are of different devices: /device:TPU:73 before, /device:TPU:2 now
where the time goes in v2:
time: 192 us; the launch traced here: 189 us
  waiting for transfers between devices  82.2 us (43%)
  starting transfers between devices  77.8 us (41%)
  Pallas kernels  22.8 us (12%)
  local copies, waits for them, and re-layouts  3.68 us (2%)
    ppermute x42, waiting for transfers between devices, shift(): lax.ppermute(value, axis, [(i, (i + step) % size) for i in range(size)])  68.2 us
    ppermute x42, starting transfers between devices, shift(): lax.ppermute(value, axis, [(i, (i + step) % size) for i in range(size)])  58.5 us
    pallas_call x10, Pallas kernels, call(): pl.pallas_call(kernel, out_shape=outs, in_specs=[SM if scalars(a) else VM...  22.5 us
    ppermute x4, starting transfers between devices, deal_heads(): return lax.ppermute(value, ('zl', 'zh'), pairs)  10.9 us
    ppermute x4, waiting for transfers between devices, deal_heads(): return lax.ppermute(value, ('zl', 'zh'), pairs)  10.7 us
    all_to_all x1, starting transfers between devices, body(): lax.all_to_all(cut, ('zh', 'c'), split_axis=0, concat_axis=0, tiled=True)  8.47 us
  transfers between devices with their start and end apart: 47, of which 20 were waited for; matrix products, arithmetic and copies ran while one was open for 1% of the time, Pallas kernels for 7%

profile of v2, /device:TPU:2, one launch (start us, length us, event | category | flops | bytes accessed | tf_op | source)
XLA Modules:
  0.0 189.1 jit_solution(12098789034204503858)
XLA Ops:
  2.6 8.5 %all-to-all-start = ((bf16[8,32,768]{2,1,0:T(8,128)(2,1)}), bf16[8,32,768]{2,1,0:T(8,128)(2,1)S(1)}, u32[]{:S(2)}, u32[]{:S(2)}) async-start(bf16[8,32,768]{2,1,0:T(8,128)(2,1)} %shard_map.130), calls=%async_computation | async-start | bytes 786432 | tf_op jit(solution)/shard_map/all_to_all | solution.py:303
  13.5 3.5 %shard_map.129 = (bf16[2,64,2048]{2,1,0:T(8,128)(2,1)}, bf16[64,2048]{1,0:T(8,128)(2,1)}, bf16[64,2048]{1,0:T(8,128)(2,1)}, bf16[64,2048]{1,0:T(8,128)(2,1)}) custom-call(s32[5]{0:T(128)S(1)} %stack.101.idx.refs_0_, bf16[128,8192]{1,0:T(8,128)(2,1)S(1)} %copy-done, f32[1,8192]{1,0:T(1,128)S(1)} %bitcast.52), custom_call_target="tpu_custom_call" | custom-call | tf_op jit(solution)/shard_map/pallas_call | solution.py:261
  18.6 2.9 %collective-permute-start.1 = (bf16[64,2048]{1,0:T(8,128)(2,1)}, bf16[64,2048]{1,0:T(8,128)(2,1)S(1)}, u32[]{:S(2)}, u32[]{:S(2)}) collective-permute-start(bf16[64,2048]{1,0:T(8,128)(2,1)} %get-tuple-element.29), channel_id=1, source_target_pairs={{0,16},{8,24},{16,0},{24,8},{1,17},{9,25},{17,1},{25,9},{2,18},{10... | collective-permute-start | bytes 786440 | tf_op jit(solution)/shard_map/ppermute | solution.py:27
  22.8 3.4 %all-to-all-done = bf16[8,32,768]{2,1,0:T(8,128)(2,1)S(1)} async-done(((bf16[8,32,768]{2,1,0:T(8,128)(2,1)}), bf16[8,32,768]{2,1,0:T(8,128)(2,1)S(1)}, u32[]{:S(2)}, u32[]{:S(2)}) %all-to-all-start) | async-done | bytes 393248 | tf_op jit(solution)/shard_map/all_to_all | solution.py:303
  27.2 6.8 %collective-permute-done.1.hb = bf16[64,2048]{1,0:T(8,128)(2,1)S(1)} collective-permute-done((bf16[64,2048]{1,0:T(8,128)(2,1)}, bf16[64,2048]{1,0:T(8,128)(2,1)S(1)}, u32[]{:S(2)}, u32[]{:S(2)}) %collective-permute-start.1) | collective-permute-done | bytes 262176 | tf_op jit(solution)/shard_map/ppermute | solution.py:27
  40.1 6.8 %collective-permute-done.9.w3 = bf16[256,768]{1,0:T(8,128)(2,1)S(1)} collective-permute-done((bf16[256,768]{1,0:T(8,128)(2,1)S(1)}, bf16[256,768]{1,0:T(8,128)(2,1)S(1)}, u32[]{:S(2)}, u32[]{:S(2)}) %collective-permute-start.9) | collective-permute-done | bytes 393248 | tf_op jit(solution)/shard_map/ppermute | solution.py:27
  48.3 3.2 %collective-permute-start.10 = (bf16[128,768]{1,0:T(8,128)(2,1)S(1)}, bf16[128,768]{1,0:T(8,128)(2,1)S(1)}, u32[]{:S(2)}, u32[]{:S(2)}) collective-permute-start(bf16[128,768]{1,0:T(8,128)(2,1)S(1)} %slice.17), channel_id=1, source_target_pairs={{0,96},{32,0},{64,32},{96,64},{1,97},{33,1},{65,33},{97,65},{2,98}... | collective-permute-start | bytes 589832 | tf_op jit(solution)/shard_map/ppermute | solution.py:27
  52.5 3.7 %collective-permute-done.5.v1 = bf16[256,768]{1,0:T(8,128)(2,1)S(1)} collective-permute-done((bf16[256,768]{1,0:T(8,128)(2,1)}, bf16[256,768]{1,0:T(8,128)(2,1)S(1)}, u32[]{:S(2)}, u32[]{:S(2)}) %collective-permute-start.5) | collective-permute-done | bytes 393248 | tf_op jit(solution)/shard_map/ppermute | solution.py:27
  64.9 3.2 %collective-permute-start.25 = (bf16[2,32,1024]{2,1,0:T(8,128)(2,1)S(1)}, bf16[2,32,1024]{2,1,0:T(8,128)(2,1)S(1)}, u32[]{:S(2)}, u32[]{:S(2)}) collective-permute-start(bf16[2,32,1024]{2,1,0:T(8,128)(2,1)S(1)} %get-tuple-element.40), channel_id=1, source_target_pairs={{0,96},{32,0},{64,32},{96,64},{1,97},{33,1},{65,33},{97,65},{2,98}... | collective-permute-start | bytes 393224 | tf_op jit(solution)/shard_map/ppermute | solution.py:27
  78.4 18.8 %collective-permute-done.29 = bf16[2,32,1024]{2,1,0:T(8,128)(2,1)S(1)} collective-permute-done((bf16[2,32,1024]{2,1,0:T(8,128)(2,1)S(1)}, bf16[2,32,1024]{2,1,0:T(8,128)(2,1)S(1)}, u32[]{:S(2)}, u32[]{:S(2)}) %collective-permute-start.29) | collective-permute-done | bytes 131104 | tf_op jit(solution)/shard_map/ppermute | solution.py:27
  104.0 4.0 %shard_map.133 = (bf16[128,512]{1,0:T(8,128)(2,1)S(1)}, bf16[128,128]{1,0:T(8,128)(2,1)}, bf16[128,128]{1,0:T(8,128)(2,1)}) custom-call(s32[5]{0:T(128)S(1)} %copy-done.8, f32[128,768]{1,0:T(8,128)S(1)} %get-tuple-element.31.p0, bf16[128,768]{1,0:T(8,128)(2,1)S(1)} %collective-permute-done.13.r1, bf16[128,768]{1,0:T(8,128)(2,1)S(1)} %collective-permute-done.14.r2, ...), custom_call_target="tpu_custom_call" | custom-call | tf_op jit(solution)/shard_map/pallas_call | solution.py:261
  117.7 3.4 %collective-permute-done.17.refs_2_ = bf16[128,512]{1,0:T(8,128)(2,1)S(1)} collective-permute-done((bf16[128,512]{1,0:T(8,128)(2,1)S(1)}, bf16[128,512]{1,0:T(8,128)(2,1)S(1)}, u32[]{:S(2)}, u32[]{:S(2)}) %collective-permute-start.17) | collective-permute-done | bytes 131104 | tf_op jit(solution)/shard_map/ppermute | solution.py:367
  121.5 2.8 %collective-permute-start.34 = (bf16[4,2,32,1024]{3,2,1,0:T(8,128)(2,1)S(1)}, bf16[4,2,32,1024]{3,2,1,0:T(8,128)(2,1)S(1)}, u32[]{:S(2)}, u32[]{:S(2)}) collective-permute-start(bf16[4,2,32,1024]{3,2,1,0:T(8,128)(2,1)S(1)} %pad_maximum_fusion.2.refs_11_), channel_id=1, source_target_pairs={{0,96},{32,0},{64,32},{96,64},{1,97},{33,1},{65,33},{97,65},{2,98}... | collective-permute-start | bytes 1572872 | tf_op jit(solution)/shard_map/ppermute | solution.py:27
  124.7 5.4 %collective-permute-start.18 = (bf16[128,512]{1,0:T(8,128)(2,1)S(1)}, bf16[128,512]{1,0:T(8,128)(2,1)S(1)}, u32[]{:S(2)}, u32[]{:S(2)}) collective-permute-start(bf16[128,512]{1,0:T(8,128)(2,1)S(1)} %get-tuple-element.37), channel_id=1, source_target_pairs={{0,4},{128,6},{2,132},{130,134},{4,0},{132,2},{6,128},{134,130},{1... | collective-permute-start | bytes 393224 | tf_op jit(solution)/shard_map/ppermute | solution.py:367
  130.1 6.8 %collective-permute-done.18.refs_3_ = bf16[128,512]{1,0:T(8,128)(2,1)S(1)} collective-permute-done((bf16[128,512]{1,0:T(8,128)(2,1)S(1)}, bf16[128,512]{1,0:T(8,128)(2,1)S(1)}, u32[]{:S(2)}, u32[]{:S(2)}) %collective-permute-start.18) | collective-permute-done | bytes 131104 | tf_op jit(solution)/shard_map/ppermute | solution.py:367
  136.9 3.7 %collective-permute-done.34.refs_14_ = bf16[4,2,32,1024]{3,2,1,0:T(8,128)(2,1)S(1)} collective-permute-done((bf16[4,2,32,1024]{3,2,1,0:T(8,128)(2,1)S(1)}, bf16[4,2,32,1024]{3,2,1,0:T(8,128)(2,1)S(1)}, u32[]{:S(2)}, u32[]{:S(2)}) %collective-permute-start.34) | collective-permute-done | bytes 524320 | tf_op jit(solution)/shard_map/ppermute | solution.py:27
  140.6 2.8 %shard_map.136 = (f32[4,4,64,128]{3,2,1,0:T(8,128)S(1)}, bf16[4,4,64,128]{3,2,1,0:T(8,128)(2,1)S(1)}) custom-call(s32[5]{0:T(128)S(1)} %copy-done.8, bf16[128,512]{1,0:T(8,128)(2,1)S(1)} %collective-permute-done.16.refs_1_, bf16[128,512]{1,0:T(8,128)(2,1)S(1)} %collective-permute-done.17.refs_2_, bf16[128,512]{1,0:T(8,128)(2,1)S(1)} %collective-permute-done.18.refs_3_, ...), custom_call_target="tpu_custom_call" | custom-call | tf_op jit(solution)/shard_map/pallas_call | solution.py:261
  144.8 5.3 %collective-permute-done.35.got = bf16[4,4,64,128]{3,2,1,0:T(8,128)(2,1)S(1)} collective-permute-done((bf16[4,4,64,128]{3,2,1,0:T(8,128)(2,1)S(1)}, bf16[4,4,64,128]{3,2,1,0:T(8,128)(2,1)S(1)}, u32[]{:S(2)}, u32[]{:S(2)}) %collective-permute-start.35) | collective-permute-done | bytes 262176 | tf_op jit(solution)/shard_map/ppermute | solution.py:27
  151.3 3.1 %collective-permute-start.37 = (bf16[2,4,64,128]{3,2,1,0:T(8,128)(2,1)S(1)}, bf16[2,4,64,128]{3,2,1,0:T(8,128)(2,1)S(1)}, u32[]{:S(2)}, u32[]{:S(2)}) collective-permute-start(bf16[2,4,64,128]{3,2,1,0:T(8,128)(2,1)S(1)} %get-tuple-element.45.refs_2_), channel_id=1, source_target_pairs={{0,6},{2,0},{4,2},{6,4},{1,7},{3,1},{5,3},{7,5},{8,14},{10,8},{12,... | collective-permute-start | bytes 393224 | tf_op jit(solution)/shard_map/ppermute | solution.py:27
  154.4 3.5 %collective-permute-done.36.refs_3_ = bf16[2,4,64,128]{3,2,1,0:T(8,128)(2,1)S(1)} collective-permute-done((bf16[2,4,64,128]{3,2,1,0:T(8,128)(2,1)S(1)}, bf16[2,4,64,128]{3,2,1,0:T(8,128)(2,1)S(1)}, u32[]{:S(2)}, u32[]{:S(2)}) %collective-permute-start.36) | collective-permute-done | bytes 131104 | tf_op jit(solution)/shard_map/ppermute | solution.py:27
  158.4 4.8 %collective-permute-start.38 = (bf16[2,4,64,128]{3,2,1,0:T(8,128)(2,1)S(1)}, bf16[2,4,64,128]{3,2,1,0:T(8,128)(2,1)S(1)}, u32[]{:S(2)}, u32[]{:S(2)}) collective-permute-start(bf16[2,4,64,128]{3,2,1,0:T(8,128)(2,1)S(1)} %get-tuple-element.45.refs_2_), channel_id=1, source_target_pairs={{0,2},{2,4},{4,6},{6,0},{1,3},{3,5},{5,7},{7,1},{8,10},{10,12},{12... | collective-permute-start | bytes 393224 | tf_op jit(solution)/shard_map/ppermute | solution.py:27
  163.2 6.8 %collective-permute-done.38.refs_5_ = bf16[2,4,64,128]{3,2,1,0:T(8,128)(2,1)S(1)} collective-permute-done((bf16[2,4,64,128]{3,2,1,0:T(8,128)(2,1)S(1)}, bf16[2,4,64,128]{3,2,1,0:T(8,128)(2,1)S(1)}, u32[]{:S(2)}, u32[]{:S(2)}) %collective-permute-start.38) | collective-permute-done | bytes 131104 | tf_op jit(solution)/shard_map/ppermute | solution.py:27
  175.9 4.1 %collective-permute-done.40.refs_7_ = bf16[2,4,64,128]{3,2,1,0:T(8,128)(2,1)S(1)} collective-permute-done((bf16[2,4,64,128]{3,2,1,0:T(8,128)(2,1)S(1)}, bf16[2,4,64,128]{3,2,1,0:T(8,128)(2,1)S(1)}, u32[]{:S(2)}, u32[]{:S(2)}) %collective-permute-start.40) | collective-permute-done | bytes 131104 | tf_op jit(solution)/shard_map/ppermute | solution.py:27
  183.8 5.4 %shard_map.138 = (bf16[128,8192]{1,0:T(8,128)(2,1)}, bf16[128,8192]{1,0:T(8,128)(2,1)}) custom-call(s32[5]{0:T(128)S(1)} %copy-done.8, bf16[2,4,64,128]{3,2,1,0:T(8,128)(2,1)S(1)} %get-tuple-element.44.refs_1_, bf16[2,4,64,128]{3,2,1,0:T(8,128)(2,1)S(1)} %get-tuple-element.45.refs_2_, bf16[2,4,64,128]{3,2,1,0:T(8,128)(2,1)S(1)} %collective-permute-done.36.refs_3_, ...), custom_call_target="tpu_custom_call" | custom-call | tf_op jit(solution)/shard_map/pallas_call | solution.py:261
  (117 shorter events, 65.7 us)
Async XLA Ops:
  2.6 23.7 %all-to-all-start = ((bf16[8,32,768]{2,1,0:T(8,128)(2,1)}), bf16[8,32,768]{2,1,0:T(8,128)(2,1)S(1)}, u32[]{:S(2)}, u32[]{:S(2)}) async-start(bf16[8,32,768]{2,1,0:T(8,128)(2,1)} %shard_map.130), calls=%async_computation | async-start | bytes 786432 | tf_op jit(solution)/shard_map/all_to_all | solution.py:303
  18.6 15.4 %collective-permute-start.1 = (bf16[64,2048]{1,0:T(8,128)(2,1)}, bf16[64,2048]{1,0:T(8,128)(2,1)S(1)}, u32[]{:S(2)}, u32[]{:S(2)}) collective-permute-start(bf16[64,2048]{1,0:T(8,128)(2,1)} %get-tuple-element.29), channel_id=1, source_target_pairs={{0,16},{8,24},{16,0},{24,8},{1,17},{9,25},{17,1},{25,9},{2,18},{10... | collective-permute-start | bytes 786440 | tf_op jit(solution)/shard_map/ppermute | solution.py:27
  21.5 12.5 %collective-permute-start.2 = (bf16[64,2048]{1,0:T(8,128)(2,1)}, bf16[64,2048]{1,0:T(8,128)(2,1)S(1)}, u32[]{:S(2)}, u32[]{:S(2)}) collective-permute-start(bf16[64,2048]{1,0:T(8,128)(2,1)} %get-tuple-element.30), channel_id=1, source_target_pairs={{0,24},{8,0},{16,8},{24,16},{1,25},{9,1},{17,9},{25,17},{2,26},{10... | collective-permute-start | bytes 786440 | tf_op jit(solution)/shard_map/ppermute | solution.py:27
  35.0 24.4 %collective-permute-start.3 = (bf16[3,64,2048]{2,1,0:T(8,128)(2,1)}, bf16[3,64,2048]{2,1,0:T(8,128)(2,1)S(1)}, u32[]{:S(2)}, u32[]{:S(2)}) collective-permute-start(bf16[3,64,2048]{2,1,0:T(8,128)(2,1)} %pad_maximum_fusion), channel_id=1, source_target_pairs={{0,1},{1,0},{2,3},{3,2},{4,5},{5,4},{6,7},{7,6},{8,9},{9,8},{10,11... | collective-permute-start | bytes 2359304 | tf_op jit(solution)/shard_map/ppermute | solution.py:27
  35.5 12.8 %collective-permute-start.7 = (bf16[256,768]{1,0:T(8,128)(2,1)S(1)}, bf16[256,768]{1,0:T(8,128)(2,1)}, u32[]{:S(2)}, u32[]{:S(2)}) collective-permute-start(bf16[256,768]{1,0:T(8,128)(2,1)S(1)} %bitcast.39), channel_id=1, source_target_pairs={{0,32},{32,64},{64,96},{96,0},{1,33},{33,65},{65,97},{97,1},{2,34}... | collective-permute-start | bytes 1179656 | tf_op jit(solution)/shard_map/ppermute | solution.py:27
  37.0 19.2 %collective-permute-start.5 = (bf16[256,768]{1,0:T(8,128)(2,1)}, bf16[256,768]{1,0:T(8,128)(2,1)S(1)}, u32[]{:S(2)}, u32[]{:S(2)}) collective-permute-start(bf16[256,768]{1,0:T(8,128)(2,1)} %collective-permute-done.4.v0), channel_id=1, source_target_pairs={{0,32},{32,64},{64,96},{96,0},{1,33},{33,65},{65,97},{97,1},{2,34}... | collective-permute-start | bytes 1179656 | tf_op jit(solution)/shard_map/ppermute | solution.py:27
  38.5 18.2 %collective-permute-start.6 = (bf16[256,768]{1,0:T(8,128)(2,1)}, bf16[256,768]{1,0:T(8,128)(2,1)S(1)}, u32[]{:S(2)}, u32[]{:S(2)}) collective-permute-start(bf16[256,768]{1,0:T(8,128)(2,1)} %collective-permute-done.4.v0), channel_id=1, source_target_pairs={{0,96},{32,0},{64,32},{96,64},{1,97},{33,1},{65,33},{97,65},{2,98}... | collective-permute-start | bytes 1179656 | tf_op jit(solution)/shard_map/ppermute | solution.py:27
  48.3 13.8 %collective-permute-start.10 = (bf16[128,768]{1,0:T(8,128)(2,1)S(1)}, bf16[128,768]{1,0:T(8,128)(2,1)S(1)}, u32[]{:S(2)}, u32[]{:S(2)}) collective-permute-start(bf16[128,768]{1,0:T(8,128)(2,1)S(1)} %slice.17), channel_id=1, source_target_pairs={{0,96},{32,0},{64,32},{96,64},{1,97},{33,1},{65,33},{97,65},{2,98}... | collective-permute-start | bytes 589832 | tf_op jit(solution)/shard_map/ppermute | solution.py:27
  56.7 13.9 %collective-permute-start.11 = (bf16[128,768]{1,0:T(8,128)(2,1)S(1)}, bf16[128,768]{1,0:T(8,128)(2,1)S(1)}, u32[]{:S(2)}, u32[]{:S(2)}) collective-permute-start(bf16[128,768]{1,0:T(8,128)(2,1)S(1)} %slice.18), channel_id=1, source_target_pairs={{0,32},{32,64},{64,96},{96,0},{1,33},{33,65},{65,97},{97,1},{2,34}... | collective-permute-start | bytes 589832 | tf_op jit(solution)/shard_map/ppermute | solution.py:27
  59.4 15.9 %collective-permute-start.23 = (bf16[2,32,1024]{2,1,0:T(8,128)(2,1)S(1)}, bf16[2,32,1024]{2,1,0:T(8,128)(2,1)S(1)}, u32[]{:S(2)}, u32[]{:S(2)}) collective-permute-start(bf16[2,32,1024]{2,1,0:T(8,128)(2,1)S(1)} %get-tuple-element.40), channel_id=1, source_target_pairs={{0,32},{32,64},{64,96},{96,0},{1,33},{33,65},{65,97},{97,1},{2,34}... | collective-permute-start | bytes 393224 | tf_op jit(solution)/shard_map/ppermute | solution.py:27
  62.1 13.9 %collective-permute-start.24 = (bf16[2,32,1024]{2,1,0:T(8,128)(2,1)S(1)}, bf16[2,32,1024]{2,1,0:T(8,128)(2,1)S(1)}, u32[]{:S(2)}, u32[]{:S(2)}) collective-permute-start(bf16[2,32,1024]{2,1,0:T(8,128)(2,1)S(1)} %get-tuple-element.40), channel_id=1, source_target_pairs={{0,64},{32,96},{64,0},{96,32},{1,65},{33,97},{65,1},{97,33},{2,66}... | collective-permute-start | bytes 393224 | tf_op jit(solution)/shard_map/ppermute | solution.py:27
  72.0 26.3 %collective-permute-start.13 = (bf16[128,768]{1,0:T(8,128)(2,1)S(1)}, bf16[128,768]{1,0:T(8,128)(2,1)S(1)}, u32[]{:S(2)}, u32[]{:S(2)}) collective-permute-start(bf16[128,768]{1,0:T(8,128)(2,1)S(1)} %get-tuple-element.32), channel_id=1, source_target_pairs={{0,24},{8,0},{16,8},{24,16},{1,25},{9,1},{17,9},{25,17},{2,26},{10... | collective-permute-start | bytes 589832 | tf_op jit(solution)/shard_map/ppermute | solution.py:27
  74.2 25.2 %collective-permute-start.14 = (bf16[128,768]{1,0:T(8,128)(2,1)S(1)}, bf16[128,768]{1,0:T(8,128)(2,1)S(1)}, u32[]{:S(2)}, u32[]{:S(2)}) collective-permute-start(bf16[128,768]{1,0:T(8,128)(2,1)S(1)} %get-tuple-element.33), channel_id=1, source_target_pairs={{0,16},{8,24},{16,0},{24,8},{1,17},{9,25},{17,1},{25,9},{2,18},{10... | collective-permute-start | bytes 589832 | tf_op jit(solution)/shard_map/ppermute | solution.py:27
  75.3 25.4 %collective-permute-start.15 = (bf16[128,768]{1,0:T(8,128)(2,1)S(1)}, bf16[128,768]{1,0:T(8,128)(2,1)S(1)}, u32[]{:S(2)}, u32[]{:S(2)}) collective-permute-start(bf16[128,768]{1,0:T(8,128)(2,1)S(1)} %get-tuple-element.34), channel_id=1, source_target_pairs={{0,8},{8,16},{16,24},{24,0},{1,9},{9,17},{17,25},{25,1},{2,10},{10... | collective-permute-start | bytes 589832 | tf_op jit(solution)/shard_map/ppermute | solution.py:27
  76.1 37.5 %collective-permute-start.26 = (bf16[4,2,32,1024]{3,2,1,0:T(8,128)(2,1)S(1)}, bf16[4,2,32,1024]{3,2,1,0:T(8,128)(2,1)S(1)}, u32[]{:S(2)}, u32[]{:S(2)}) collective-permute-start(bf16[4,2,32,1024]{3,2,1,0:T(8,128)(2,1)S(1)} %pad_maximum_fusion.1.refs_7_), channel_id=1, source_target_pairs={{0,8},{8,16},{16,24},{24,0},{1,9},{9,17},{17,25},{25,1},{2,10},{10... | collective-permute-start | bytes 1572872 | tf_op jit(solution)/shard_map/ppermute | solution.py:27
  77.9 19.2 %collective-permute-start.29 = (bf16[2,32,1024]{2,1,0:T(8,128)(2,1)S(1)}, bf16[2,32,1024]{2,1,0:T(8,128)(2,1)S(1)}, u32[]{:S(2)}, u32[]{:S(2)}) collective-permute-start(bf16[2,32,1024]{2,1,0:T(8,128)(2,1)S(1)} %get-tuple-element.41), channel_id=1, source_target_pairs={{0,8},{8,16},{16,24},{24,0},{1,9},{9,17},{17,25},{25,1},{2,10},{10... | collective-permute-start | bytes 393224 | tf_op jit(solution)/shard_map/ppermute | solution.py:27
  98.3 12.8 %collective-permute-start.31 = (bf16[2,32,1024]{2,1,0:T(8,128)(2,1)S(1)}, bf16[2,32,1024]{2,1,0:T(8,128)(2,1)S(1)}, u32[]{:S(2)}, u32[]{:S(2)}) collective-permute-start(bf16[2,32,1024]{2,1,0:T(8,128)(2,1)S(1)} %get-tuple-element.41), channel_id=1, source_target_pairs={{0,24},{8,0},{16,8},{24,16},{1,25},{9,1},{17,9},{25,17},{2,26},{10... | collective-permute-start | bytes 393224 | tf_op jit(solution)/shard_map/ppermute | solution.py:27
  99.5 24.9 %collective-permute-start.27 = (bf16[4,2,32,1024]{3,2,1,0:T(8,128)(2,1)S(1)}, bf16[4,2,32,1024]{3,2,1,0:T(8,128)(2,1)S(1)}, u32[]{:S(2)}, u32[]{:S(2)}) collective-permute-start(bf16[4,2,32,1024]{3,2,1,0:T(8,128)(2,1)S(1)} %pad_maximum_fusion.1.refs_7_), channel_id=1, source_target_pairs={{0,16},{8,24},{16,0},{24,8},{1,17},{9,25},{17,1},{25,9},{2,18},{10... | collective-permute-start | bytes 1572872 | tf_op jit(solution)/shard_map/ppermute | solution.py:27
  100.7 23.9 %collective-permute-start.28 = (bf16[4,2,32,1024]{3,2,1,0:T(8,128)(2,1)S(1)}, bf16[4,2,32,1024]{3,2,1,0:T(8,128)(2,1)S(1)}, u32[]{:S(2)}, u32[]{:S(2)}) collective-permute-start(bf16[4,2,32,1024]{3,2,1,0:T(8,128)(2,1)S(1)} %pad_maximum_fusion.1.refs_7_), channel_id=1, source_target_pairs={{0,24},{8,0},{16,8},{24,16},{1,25},{9,1},{17,9},{25,17},{2,26},{10... | collective-permute-start | bytes 1572872 | tf_op jit(solution)/shard_map/ppermute | solution.py:27
  115.9 21.0 %collective-permute-start.32 = (bf16[4,2,32,1024]{3,2,1,0:T(8,128)(2,1)S(1)}, bf16[4,2,32,1024]{3,2,1,0:T(8,128)(2,1)S(1)}, u32[]{:S(2)}, u32[]{:S(2)}) collective-permute-start(bf16[4,2,32,1024]{3,2,1,0:T(8,128)(2,1)S(1)} %pad_maximum_fusion.2.refs_11_), channel_id=1, source_target_pairs={{0,32},{32,64},{64,96},{96,0},{1,33},{33,65},{65,97},{97,1},{2,34}... | collective-permute-start | bytes 1572872 | tf_op jit(solution)/shard_map/ppermute | solution.py:27
  121.1 15.8 %collective-permute-start.33 = (bf16[4,2,32,1024]{3,2,1,0:T(8,128)(2,1)S(1)}, bf16[4,2,32,1024]{3,2,1,0:T(8,128)(2,1)S(1)}, u32[]{:S(2)}, u32[]{:S(2)}) collective-permute-start(bf16[4,2,32,1024]{3,2,1,0:T(8,128)(2,1)S(1)} %pad_maximum_fusion.2.refs_11_), channel_id=1, source_target_pairs={{0,64},{32,96},{64,0},{96,32},{1,65},{33,97},{65,1},{97,33},{2,66}... | collective-permute-start | bytes 1572872 | tf_op jit(solution)/shard_map/ppermute | solution.py:27
  121.5 19.1 %collective-permute-start.34 = (bf16[4,2,32,1024]{3,2,1,0:T(8,128)(2,1)S(1)}, bf16[4,2,32,1024]{3,2,1,0:T(8,128)(2,1)S(1)}, u32[]{:S(2)}, u32[]{:S(2)}) collective-permute-start(bf16[4,2,32,1024]{3,2,1,0:T(8,128)(2,1)S(1)} %pad_maximum_fusion.2.refs_11_), channel_id=1, source_target_pairs={{0,96},{32,0},{64,32},{96,64},{1,97},{33,1},{65,33},{97,65},{2,98}... | collective-permute-start | bytes 1572872 | tf_op jit(solution)/shard_map/ppermute | solution.py:27
  124.4 16.3 %collective-permute-start.20 = (bf16[3,128,512]{2,1,0:T(8,128)(2,1)S(1)}, bf16[3,128,512]{2,1,0:T(8,128)(2,1)S(1)}, u32[]{:S(2)}, u32[]{:S(2)}) collective-permute-start(bf16[3,128,512]{2,1,0:T(8,128)(2,1)S(1)} %pad_maximum_fusion.4), channel_id=1, source_target_pairs={{0,1},{1,0},{2,3},{3,2},{4,5},{5,4},{6,7},{7,6},{8,9},{9,8},{10,11... | collective-permute-start | bytes 1179656 | tf_op jit(solution)/shard_map/ppermute | solution.py:27
  158.3 25.4 %collective-permute-start.42 = (bf16[4,2,4,64,128]{4,3,2,1,0:T(8,128)(2,1)S(1)}, bf16[4,2,4,64,128]{4,3,2,1,0:T(8,128)(2,1)S(1)}, u32[]{:S(2)}, u32[]{:S(2)}) collective-permute-start(bf16[4,2,4,64,128]{4,3,2,1,0:T(8,128)(2,1)S(1)} %pad_maximum_fusion.3), channel_id=1, source_target_pairs={{0,1},{1,0},{2,3},{3,2},{4,5},{5,4},{6,7},{7,6},{8,9},{9,8},{10,11... | collective-permute-start | bytes 1572872 | tf_op jit(solution)/shard_map/ppermute | solution.py:27
  (33 other events, 435.2 us)
